TPU v7x, 16 devices: a 4x2x1 block of a 4x4x8 slice. The times are simulated.
16 devices in a mesh: dp: 2 (over y, z), ep: 8 (over x, core).
Axes of the slice: x: 4, y: 2, z: 1, core: 2. Of those that a mesh axis runs over, the one named last changes fastest.
The devices are a block of a 4x4x8 slice.
Arguments:
- tokens_a: bfloat16 [8192, 2048], P(('dp', 'ep')), parts along dimension 0
- experts_a: int32 [8192, 6], P(('dp', 'ep')), parts along dimension 0
- slots_a: int32 [8192, 6], P(('dp', 'ep')), parts along dimension 0
- gates_a: bfloat16 [8192, 6], P(('dp', 'ep')), parts along dimension 0
- tokens_b: bfloat16 [8192, 2048], P(('dp', 'ep')), parts along dimension 0
- experts_b: int32 [8192, 6], P(('dp', 'ep')), parts along dimension 0
- slots_b: int32 [8192, 6], P(('dp', 'ep')), parts along dimension 0
- gates_b: bfloat16 [8192, 6], P(('dp', 'ep')), parts along dimension 0
- attn_gain: bfloat16 [2048], replicated
- w_query: bfloat16 [2048, 16, 128], replicated
- w_key: bfloat16 [2048, 16, 128], replicated
- w_value: bfloat16 [2048, 16, 128], replicated
- w_out: bfloat16 [16, 128, 2048], replicated
- moe_gain: bfloat16 [2048], replicated
- w_gate: bfloat16 [64, 2048, 1408], P('ep')
- w_up: bfloat16 [64, 2048, 1408], P('ep')
- w_down: bfloat16 [64, 1408, 2048], P('ep')
Outputs:
- output 1: bfloat16 [8192, 2048], P(('dp', 'ep')), parts along dimension 0
- output 2: bfloat16 [8192, 2048], P(('dp', 'ep')), parts along dimension 0
There are 2 independent parts. A program takes and returns all parts, laid end to end along the dimension named above; an argument that names none is the same for every part.
All inputs are finite; a program needn't handle non-finite values.
Results may differ from a plain program's by a relative error of at most 0.0125727.
Values are sent between devices in bfloat16 or wider.
A program may use at most 768 MiB of HBM per device.

v0:
```python
import jax
import jax.numpy as jnp
from jax import lax
from jax.sharding import PartitionSpec as P

NORM_EPS = 1e-6
MASK_VALUE = -1e30


def rms_norm(rows, gain_vec):
    rows_f = rows.astype(jnp.float32)
    inv_rms = lax.rsqrt(jnp.mean(rows_f * rows_f, axis=-1, keepdims=True) + NORM_EPS)
    return (rows_f * inv_rms * gain_vec.astype(jnp.float32)).astype(jnp.bfloat16)


def attention_block(sequence, attn_gain, w_query, w_key, w_value, w_out):
    seq_len = sequence.shape[0]
    normed = rms_norm(sequence, attn_gain)
    query = jnp.einsum("td,dhe->the", normed, w_query, preferred_element_type=jnp.float32).astype(jnp.bfloat16)
    keys = jnp.einsum("td,dhe->the", normed, w_key, preferred_element_type=jnp.float32).astype(jnp.bfloat16)
    values = jnp.einsum("td,dhe->the", normed, w_value, preferred_element_type=jnp.float32).astype(jnp.bfloat16)
    scores = jnp.einsum("qhe,khe->hqk", query, keys, preferred_element_type=jnp.float32) * (w_query.shape[2] ** -0.5)
    causal = lax.broadcasted_iota(jnp.int32, (seq_len, seq_len), 0) >= lax.broadcasted_iota(jnp.int32, (seq_len, seq_len), 1)
    scores = jnp.where(causal[None, :, :], scores, MASK_VALUE)
    attn_prob = jax.nn.softmax(scores, axis=-1).astype(jnp.bfloat16)
    context = jnp.einsum("hqk,khe->qhe", attn_prob, values, preferred_element_type=jnp.float32).astype(jnp.bfloat16)
    attn_out = jnp.einsum("qhe,hed->qd", context, w_out, preferred_element_type=jnp.float32)
    return (sequence.astype(jnp.float32) + attn_out).astype(jnp.bfloat16)


def capacity_of(seq_len, top_k, experts_total):
    return 8 * max(1, (seq_len * top_k) // (4 * experts_total))


def dispatch_rows(normed, dest_row, experts_total, capacity):
    seq_len, model_dim = normed.shape
    top_k = dest_row.shape[0] // seq_len
    token_of = jnp.arange(seq_len * top_k, dtype=jnp.int32) // top_k
    source = jnp.full((experts_total * capacity,), seq_len, jnp.int32).at[dest_row].set(token_of, mode="drop")
    return jnp.take(normed, source, axis=0, mode="fill", fill_value=0).reshape(experts_total, capacity, model_dim)


def combine_rows(residual, returned, dest_row, gates):
    seq_len, model_dim = residual.shape
    top_k = gates.shape[1]
    picked = jnp.take(returned.reshape(-1, model_dim), dest_row, axis=0, mode="fill", fill_value=0).reshape(seq_len, top_k, model_dim)
    mixed_sum = jnp.einsum("tk,tkd->td", gates, picked, preferred_element_type=jnp.float32)
    return (residual.astype(jnp.float32) + mixed_sum).astype(jnp.bfloat16)


def expert_ffn(received, w_gate, w_up, w_down):
    gate_act = jnp.einsum("pecd,edf->pecf", received, w_gate, preferred_element_type=jnp.float32)
    up_act = jnp.einsum("pecd,edf->pecf", received, w_up, preferred_element_type=jnp.float32)
    hidden = (jax.nn.silu(gate_act) * up_act).astype(jnp.bfloat16)
    return jnp.einsum("pecf,efd->pecd", hidden, w_down, preferred_element_type=jnp.float32).astype(jnp.bfloat16)


def moe_layer(tokens, experts, slots, gates, attn_gain, w_query, w_key, w_value, w_out, moe_gain, w_gate, w_up, w_down, group):
    seq_len, model_dim = tokens.shape
    local_experts = w_gate.shape[0]
    experts_total = local_experts * group
    capacity = capacity_of(seq_len, experts.shape[1], experts_total)
    residual = attention_block(tokens, attn_gain, w_query, w_key, w_value, w_out)
    normed = rms_norm(residual, moe_gain)
    dest_row = jnp.where(slots >= 0, experts * capacity + slots, experts_total * capacity).reshape(-1)
    dispatched = dispatch_rows(normed, dest_row, experts_total, capacity)
    received = lax.all_to_all(dispatched, "ep", 0, 0, tiled=True).reshape(group, local_experts, capacity, model_dim)
    expert_out = expert_ffn(received, w_gate, w_up, w_down).reshape(experts_total, capacity, model_dim)
    returned = lax.all_to_all(expert_out, "ep", 0, 0, tiled=True)
    return combine_rows(residual, returned, dest_row, gates)


def solution(mesh):
    group = mesh.shape["ep"]
    row_spec = P(("dp", "ep"), None)
    full_spec = P(None, None, None)
    gain_spec = P(None)
    expert_spec = P("ep", None, None)
    in_specs = (row_spec, row_spec, row_spec, row_spec, row_spec, row_spec, row_spec, row_spec, gain_spec, full_spec, full_spec, full_spec, full_spec, gain_spec, expert_spec, expert_spec, expert_spec)

    def device_fn(tokens_a, experts_a, slots_a, gates_a, tokens_b, experts_b, slots_b, gates_b, attn_gain, w_query, w_key, w_value, w_out, moe_gain, w_gate, w_up, w_down):
        out_a = moe_layer(tokens_a, experts_a, slots_a, gates_a, attn_gain, w_query, w_key, w_value, w_out, moe_gain, w_gate, w_up, w_down, group)
        out_b = moe_layer(tokens_b, experts_b, slots_b, gates_b, attn_gain, w_query, w_key, w_value, w_out, moe_gain, w_gate, w_up, w_down, group)
        return out_a, out_b

    return jax.shard_map(device_fn, mesh=mesh, in_specs=in_specs, out_specs=(row_spec, row_spec), check_vma=False)
```

profile of v0, /device:TPU:112, one launch (start us, length us, event | category | flops | bytes accessed | tf_op | source)
XLA Modules:
  0.0 1432.7 jit_solution(2293487514870725760)
XLA Ops:
  0.7 0.7 convert_element_type.103
  1.4 2.2 fusion.64
  3.7 10.1 fusion.48
  13.8 7.6 fusion.52
  21.9 7.4 fusion.50
  29.3 7.4 fusion.54
  37.3 12.3 scatter_custom_fusion.1
  49.7 0.6 compare_and_fusion
  50.3 4.2 copy.77
  54.5 12.8 fusion.79
  67.4 17.2 %fusion.87 = f32[16,512,512]{1,2,0:T(8,128)} fusion(bf16[2048,16,128]{2,1,0:T(8,128)(2,1)} %param.31, bf16[512,16,128]{2,0,1:T(8,128)(2,1)} %fusion.50, bf16[512,2048]{1,0:T(8,128)(2,1)} %param.21, f32[2048]{0:T(1024)S(1)} %convert_element_type.103, f32[512]{0:T(512)S(1)} %add_rsqrt_fusion.3), kind=kOutput, calls=%fused_computation.113 | convolution fusion | flops 5373952000 | bytes 29370368 | tf_op jit(solution)/shard_map/qhe,khe->hqk/dot_general | solution.py:22
  84.6 18.0 %fusion.118 = (f32[16,512]{1,0:T(8,128)S(1)}, f32[16,512,512]{1,2,0:T(8,128)}) fusion(f32[16,512,512]{1,2,0:T(8,128)} %fusion.79, pred[512,512]{0,1:T(8,128)(4,1)S(1)} %iota_compare_fusion), kind=kOutput, calls=%fused_computation.153 | output fusion | flops 25166336 | bytes 33849344 | tf_op jit(solution)/shard_map/sub | solution.py:25
  102.6 18.2 %fusion.117 = (f32[16,512]{1,0:T(8,128)S(1)}, f32[16,512,512]{1,2,0:T(8,128)}) fusion(f32[16,512,512]{1,2,0:T(8,128)} %fusion.87, pred[512,512]{0,1:T(8,128)(4,1)S(1)} %iota_compare_fusion), kind=kOutput, calls=%fused_computation.152 | output fusion | flops 25166336 | bytes 33849344 | tf_op jit(solution)/shard_map/sub | solution.py:25
  120.8 4.3 copy.78
  125.0 14.8 %fusion.68 = (f32[512]{0:T(512)S(1)}, bf16[512,2048]{1,0:T(8,128)(2,1)}) fusion(bf16[16,128,2048]{2,1,0:T(8,128)(2,1)} %param.33, bf16[512,2048]{1,0:T(8,128)(2,1)S(1)} %copy-done.6, f32[16,512,512]{1,2,0:T(8,128)} %get-tuple-element.9, f32[16,512]{1,0:T(8,128)S(1)} %get-tuple-element.8, bf16[512,16,128]{2,1,0:T(8,128)(2,1)} %copy.77), kind=kOutput, calls=%fused_computation.96 | convolution fusion | flops 5383388672 | bytes 31492096 | tf_op jit(solution)/shard_map/qhe,hed->qd/dot_general | solution.py:27
  139.9 15.4 %fusion.60 = (f32[512]{0:T(512)S(1)}, bf16[512,2048]{1,0:T(8,128)(2,1)}) fusion(bf16[16,128,2048]{2,1,0:T(8,128)(2,1)} %param.33, bf16[512,2048]{1,0:T(8,128)(2,1)} %param.21, f32[16,512,512]{1,2,0:T(8,128)} %get-tuple-element.7, f32[16,512]{1,0:T(8,128)S(1)} %get-tuple-element.6, bf16[512,16,128]{2,1,0:T(8,128)(2,1)} %copy.78), kind=kOutput, calls=%fused_computation.88 | convolution fusion | flops 5383388672 | bytes 31492096 | tf_op jit(solution)/shard_map/qhe,hed->qd/dot_general | solution.py:27
  155.2 4.4 fusion.70
  159.7 48.2 %gather_fusion.2 = bf16[6144,2048]{1,0:T(8,128)(2,1)} fusion(bf16[512,2048]{1,0:T(8,128)(2,1)} %get-tuple-element.4, s32[6144]{0:T(1024)S(1)} %fusion.103), kind=kCustom, calls=%fused_computation.2.clone | custom fusion | bytes 50356224 | tf_op jit(solution)/shard_map/jit(_take)/gather | solution.py:40
  207.9 21.6 %broadcast_select_fusion = bf16[6144,2048]{1,0:T(8,128)(2,1)} fusion(bf16[6144,2048]{1,0:T(8,128)(2,1)} %gather_fusion.2, pred[6144]{0:T(1024)(128)(4,1)S(1)} %copy-done.8), kind=kLoop, calls=%fused_computation.36 | loop fusion | flops 12582912 | bytes 50337792 | tf_op jit(solution)/shard_map/jit(_take)/select_n | solution.py:40
  229.5 6.8 all-to-all-start.2
  236.7 12.0 scatter_custom_fusion
  248.7 30.7 %gather_fusion = bf16[6144,2048]{1,0:T(8,128)(2,1)} fusion(bf16[512,2048]{1,0:T(8,128)(2,1)S(1)} %get-tuple-element.5, s32[6144]{0:T(1024)S(1)} %fusion.102), kind=kCustom, calls=%fused_computation.clone | custom fusion | bytes 50356224 | tf_op jit(solution)/shard_map/jit(_take)/gather | solution.py:40
  279.5 21.6 %broadcast_select_fusion.1 = bf16[6144,2048]{1,0:T(8,128)(2,1)} fusion(bf16[6144,2048]{1,0:T(8,128)(2,1)} %gather_fusion, pred[6144]{0:T(1024)(128)(4,1)S(1)} %compare_and_fusion.1), kind=kLoop, calls=%fused_computation.37 | loop fusion | flops 12582912 | bytes 50337792 | tf_op jit(solution)/shard_map/jit(_take)/select_n | solution.py:40
  301.0 209.6 %all-to-all-done.2 = bf16[64,96,2048]{2,1,0:T(8,128)(2,1)} async-done(((bf16[64,96,2048]{2,1,0:T(8,128)(2,1)}), bf16[64,96,2048]{2,1,0:T(8,128)(2,1)}, u32[]{:S(2)}, u32[]{:S(2)}) %all-to-all-start.2) | async-done | bytes 25165856 | tf_op jit(solution)/shard_map/all_to_all | solution.py:67
  510.7 7.1 all-to-all-start
  517.7 49.0 %fusion.6 = f32[8,8,96,1408]{3,2,1,0:T(8,128)} fusion(bf16[8,2048,1408]{2,1,0:T(8,128)(2,1)} %param.36, bf16[8,8,96,2048]{3,2,1,0:T(8,128)(2,1)} %bitcast.24), kind=kOutput, calls=%fused_computation.12 | convolution fusion | flops 35433480192 | bytes 105906176 | tf_op jit(solution)/shard_map/pecd,edf->pecf/dot_general | solution.py:53
  566.8 58.6 %fusion.14 = bf16[8,8,96,1408]{3,2,0,1:T(8,128)(2,1)} fusion(f32[8,8,96,1408]{3,2,1,0:T(8,128)} %fusion.6, bf16[8,2048,1408]{2,1,0:T(8,128)(2,1)} %param.35, bf16[8,8,96,2048]{3,2,1,0:T(8,128)(2,1)} %bitcast.24), kind=kOutput, calls=%fused_computation.21 | convolution fusion | flops 35485384704 | bytes 123207680 | tf_op jit(solution)/shard_map/pecd,edf->pecf/dot_general | solution.py:52
  625.4 48.0 %convert_bitcast_fusion = bf16[8,8,96,2048]{3,2,0,1:T(8,128)(2,1)} fusion(bf16[8,8,96,1408]{3,2,0,1:T(8,128)(2,1)} %fusion.14, bf16[8,1408,2048]{2,1,0:T(8,128)(2,1)} %param.37), kind=kOutput, calls=%fused_computation.34 | convolution fusion | flops 35446063104 | bytes 88604672 | tf_op jit(solution)/shard_map/pecf,efd->pecd/dot_general | solution.py:55
  673.4 21.1 %copy.26 = bf16[8,8,96,2048]{3,2,1,0:T(8,128)(2,1)} copy(bf16[8,8,96,2048]{3,2,0,1:T(8,128)(2,1)} %convert_bitcast_fusion) | data formatting | bytes 50331648 | tf_op jit(solution)/shard_map/convert_element_type | solution.py:55
  694.4 97.5 %all-to-all-done = bf16[64,96,2048]{2,1,0:T(8,128)(2,1)} async-done(((bf16[64,96,2048]{2,1,0:T(8,128)(2,1)}), bf16[64,96,2048]{2,1,0:T(8,128)(2,1)}, u32[]{:S(2)}, u32[]{:S(2)}) %all-to-all-start) | async-done | bytes 25165856 | tf_op jit(solution)/shard_map/all_to_all | solution.py:67
  791.9 6.9 all-to-all-start.3
  798.9 49.0 %fusion.8 = f32[8,8,96,1408]{3,2,1,0:T(8,128)} fusion(bf16[8,2048,1408]{2,1,0:T(8,128)(2,1)} %param.36, bf16[8,8,96,2048]{3,2,1,0:T(8,128)(2,1)} %bitcast.5), kind=kOutput, calls=%fused_computation.14 | convolution fusion | flops 35433480192 | bytes 105906176 | tf_op jit(solution)/shard_map/pecd,edf->pecf/dot_general | solution.py:53
  847.9 58.7 %fusion.18 = bf16[8,8,96,1408]{3,2,0,1:T(8,128)(2,1)} fusion(f32[8,8,96,1408]{3,2,1,0:T(8,128)} %fusion.8, bf16[8,2048,1408]{2,1,0:T(8,128)(2,1)} %param.35, bf16[8,8,96,2048]{3,2,1,0:T(8,128)(2,1)} %bitcast.5), kind=kOutput, calls=%fused_computation.28 | convolution fusion | flops 35485384704 | bytes 123207680 | tf_op jit(solution)/shard_map/pecd,edf->pecf/dot_general | solution.py:52
  906.6 48.1 %convert_bitcast_fusion.1 = bf16[8,8,96,2048]{3,2,0,1:T(8,128)(2,1)} fusion(bf16[8,8,96,1408]{3,2,0,1:T(8,128)(2,1)} %fusion.18, bf16[8,1408,2048]{2,1,0:T(8,128)(2,1)} %param.37), kind=kOutput, calls=%fused_computation.35 | convolution fusion | flops 35446063104 | bytes 88604672 | tf_op jit(solution)/shard_map/pecf,efd->pecd/dot_general | solution.py:55
  954.7 21.0 %copy.22 = bf16[8,8,96,2048]{3,2,1,0:T(8,128)(2,1)} copy(bf16[8,8,96,2048]{3,2,0,1:T(8,128)(2,1)} %convert_bitcast_fusion.1) | data formatting | bytes 50331648 | tf_op jit(solution)/shard_map/convert_element_type | solution.py:55
  975.7 97.3 %all-to-all-done.3 = bf16[64,96,2048]{2,1,0:T(8,128)(2,1)} async-done(((bf16[64,96,2048]{2,1,0:T(8,128)(2,1)}), bf16[64,96,2048]{2,1,0:T(8,128)(2,1)}, u32[]{:S(2)}, u32[]{:S(2)}) %all-to-all-start.3) | async-done | bytes 25165856 | tf_op jit(solution)/shard_map/all_to_all | solution.py:69
  1073.0 7.2 all-to-all-start.1
  1081.1 35.2 %gather_fusion.3 = bf16[3072,2048]{1,0:T(8,128)(2,1)} fusion(bf16[6144,2048]{1,0:T(8,128)(2,1)} %bitcast.32, s32[3072]{0:T(1024)S(1)} %fusion.112), kind=kCustom, calls=%fused_computation.3.clone | custom fusion | bytes 25178112 | tf_op jit(solution)/shard_map/jit(_take)/gather | solution.py:46
  1116.3 11.1 broadcast_select_fusion.2
  1127.4 20.3 %reshape.168 = bf16[512,6,2048]{2,1,0:T(8,128)(2,1)} reshape(bf16[3072,2048]{1,0:T(8,128)(2,1)} %broadcast_select_fusion.2) | data formatting | bytes 25165824 | tf_op jit(solution)/shard_map/reshape | solution.py:46
  1147.7 8.7 fusion.120
  1156.5 2.9 fusion.71
  1159.4 195.0 %all-to-all-done.1 = bf16[64,96,2048]{2,1,0:T(8,128)(2,1)} async-done(((bf16[64,96,2048]{2,1,0:T(8,128)(2,1)}), bf16[64,96,2048]{2,1,0:T(8,128)(2,1)}, u32[]{:S(2)}, u32[]{:S(2)}) %all-to-all-start.1) | async-done | bytes 25165856 | tf_op jit(solution)/shard_map/all_to_all | solution.py:69
  1354.4 35.2 %gather_fusion.1 = bf16[3072,2048]{1,0:T(8,128)(2,1)} fusion(bf16[6144,2048]{1,0:T(8,128)(2,1)} %bitcast.16, s32[3072]{0:T(1024)S(1)} %fusion.111), kind=kCustom, calls=%fused_computation.1.clone | custom fusion | bytes 25178112 | tf_op jit(solution)/shard_map/jit(_take)/gather | solution.py:46
  1389.7 11.0 broadcast_select_fusion.3
  1400.7 20.4 %reshape.161 = bf16[512,6,2048]{2,1,0:T(8,128)(2,1)} reshape(bf16[3072,2048]{1,0:T(8,128)(2,1)} %broadcast_select_fusion.3) | data formatting | bytes 25165824 | tf_op jit(solution)/shard_map/reshape | solution.py:46
  1421.0 8.6 fusion.119
  1429.6 2.9 fusion.63
  (70 shorter events, 2.4 us)
Async XLA Ops:
  1.4 12.3 slice-start.2
  3.6 10.1 copy-start.6
  3.7 10.1 slice-start.3
  3.7 18.2 %slice-start = ((s8[8388608]{0:T(1024)(128)(4,1)}), s8[4194304]{0:T(1024)(128)(4,1)S(1)}, s32[]{:S(2)}) async-start(s8[8388608]{0:T(1024)(128)(4,1)} %bitcast.127), calls=%async_computation.4 | async-start | bytes 8388608
  13.8 7.6 copy-start.7
  13.8 8.1 slice-start.1
  29.3 7.4 copy-start.9
  29.3 7.4 copy-start.10
  36.7 0.6 copy-start.13
  36.9 30.5 %copy-start.2 = (s32[512,6]{1,0:T(8,128)}, s32[512,6]{1,0:T(8,128)S(1)}, u32[]{:S(2)}) copy-start(s32[512,6]{1,0:T(8,128)S(1)} %copy.23) | copy-start | bytes 36868
  102.6 22.4 %copy-start.16 = (bf16[2048]{0:T(1024)(128)(2,1)S(1)}, bf16[2048]{0:T(1024)(128)(2,1)}, u32[]{:S(2)}) copy-start(bf16[2048]{0:T(1024)(128)(2,1)} %param.34) | copy-start | bytes 12292
  159.7 48.2 %copy-start.8 = (pred[6144]{0:T(1024)(128)(4,1)S(1)}, pred[6144]{0:T(1024)(128)(4,1)}, u32[]{:S(2)}) copy-start(pred[6144]{0:T(1024)(128)(4,1)} %compare_and_fusion) | copy-start | bytes 18436
  229.5 6.8 copy-start.11
  229.5 6.8 copy-start.12
  229.5 281.1 %all-to-all-start.2 = ((bf16[64,96,2048]{2,1,0:T(8,128)(2,1)}), bf16[64,96,2048]{2,1,0:T(8,128)(2,1)}, u32[]{:S(2)}, u32[]{:S(2)}) async-start(bf16[64,96,2048]{2,1,0:T(8,128)(2,1)} %bitcast.120), calls=%async_computation.2 | async-start | bytes 50331648 | tf_op jit(solution)/shard_map/all_to_all | solution.py:67
  236.5 43.0 %copy-start.4 = (s32[512,6]{1,0:T(8,128)}, s32[512,6]{1,0:T(8,128)S(1)}, u32[]{:S(2)}) copy-start(s32[512,6]{1,0:T(8,128)S(1)} %copy.19) | copy-start | bytes 36868
  510.7 281.2 %all-to-all-start = ((bf16[64,96,2048]{2,1,0:T(8,128)(2,1)}), bf16[64,96,2048]{2,1,0:T(8,128)(2,1)}, u32[]{:S(2)}, u32[]{:S(2)}) async-start(bf16[64,96,2048]{2,1,0:T(8,128)(2,1)} %bitcast.121), calls=%async_computation | async-start | bytes 50331648 | tf_op jit(solution)/shard_map/all_to_all | solution.py:67
  791.9 281.1 %all-to-all-start.3 = ((bf16[64,96,2048]{2,1,0:T(8,128)(2,1)}), bf16[64,96,2048]{2,1,0:T(8,128)(2,1)}, u32[]{:S(2)}, u32[]{:S(2)}) async-start(bf16[64,96,2048]{2,1,0:T(8,128)(2,1)} %bitcast.122), calls=%async_computation.3 | async-start | bytes 50331648 | tf_op jit(solution)/shard_map/all_to_all | solution.py:69
  1073.0 7.3 copy-start.3
  1073.0 7.4 copy-start.5
  1073.0 7.6 copy-start.14
  1073.0 7.8 copy-start.15
  1073.0 281.4 %all-to-all-start.1 = ((bf16[64,96,2048]{2,1,0:T(8,128)(2,1)}), bf16[64,96,2048]{2,1,0:T(8,128)(2,1)}, u32[]{:S(2)}, u32[]{:S(2)}) async-start(bf16[64,96,2048]{2,1,0:T(8,128)(2,1)} %bitcast.119), calls=%async_computation.1 | async-start | bytes 50331648 | tf_op jit(solution)/shard_map/all_to_all | solution.py:69
  1147.7 8.8 copy-start.1
  1421.0 8.6 copy-start
where the time goes:
time: 1440 us; the launch traced here: 1430 us
  waiting for transfers between devices  599 us (42%)
  matrix products  421 us (29%)
  local copies, waits for them, and re-layouts  267 us (19%)
  other arithmetic  116 us (8%)
  starting transfers between devices  28 us (2%)
    all_to_all x2, waiting for transfers between devices, moe_layer(): lax.all_to_all(dispatched, 'ep', 0, 0, tiled=True)  307 us
    all_to_all x2, waiting for transfers between devices, moe_layer(): returned = lax.all_to_all(expert_out, 'ep', 0, 0, tiled=True)  292 us
    dot_general x2, matrix products, expert_ffn(): jnp.einsum('pecd,edf->pecf', received, w_gate, preferred_element_type=jnp...  117 us
    dot_general x2, matrix products, expert_ffn(): jnp.einsum('pecd,edf->pecf', received, w_up, preferred_element_type=jnp.f...  98.1 us
    dot_general x2, matrix products, expert_ffn(): jnp.einsum('pecf,efd->pecd', hidden, w_down, preferred_element_type=jnp.f...  96.1 us
    gather x2, local copies, waits for them, and re-layouts, dispatch_rows(): jnp.take(normed, source, axis=0, mode='fill', fill_value=0)  79 us
    gather x2, local copies, waits for them, and re-layouts, combine_rows(): jnp.take(returned.reshape(-1, model_dim), dest_row, axis=0, mode='fill',...  70.4 us
    select_n x2, other arithmetic, dispatch_rows(): jnp.take(normed, source, axis=0, mode='fill', fill_value=0)  43.2 us
  transfers between devices with their start and end apart: 4, of which 4 were waited for; matrix products, arithmetic and copies ran while one was open for 35% of the time, Pallas kernels for 0%

commit v1 on v0

v1 whole, which is shorter than its diff:
```python
import functools

import jax
import jax.numpy as jnp
from jax import lax
from jax.experimental import pallas as pl
from jax.experimental.pallas import tpu as pltpu
from jax.sharding import PartitionSpec as P

NORM_EPS = 1e-6
MASK_VALUE = -1e30
BLOCK = 16
TILE = 256
COUNT_ROW = 6
MOST_ROW = 7
BASE = 1024
VMEM_LIMIT = 62 * 1024 * 1024
F32 = jnp.float32
BF16 = jnp.bfloat16
I32 = jnp.int32


def rms_rows(rows_f, gain_f):
    inv_rms = lax.rsqrt(jnp.mean(rows_f * rows_f, axis=-1, keepdims=True) + NORM_EPS)
    return (rows_f * inv_rms * gain_f).astype(BF16)


def route_kernel(local_experts, top_k, experts_ref, slots_ref, table_ref, exact_ref):
    seq_len = experts_ref.shape[1]
    lanes = 128
    ids = experts_ref[0]
    slot = slots_ref[0]
    lane = lax.broadcasted_iota(I32, (seq_len, lanes), 1)
    hits = [jnp.where((ids[:, j : j + 1] == lane) & (slot[:, j : j + 1] >= 0), 1.0, 0.0) for j in range(top_k)]
    kept = functools.reduce(lambda a, b: a + b, hits)
    row = lax.broadcasted_iota(I32, (seq_len, seq_len), 0)
    col = lax.broadcasted_iota(I32, (seq_len, seq_len), 1)
    before = jnp.where(col < row, 1.0, 0.0).astype(BF16)
    rank = jnp.dot(before, kept.astype(BF16), preferred_element_type=F32)
    count8 = jnp.broadcast_to(jnp.sum(kept, axis=0, keepdims=True), (8, lanes))
    padded8 = ((count8.astype(I32) + (BLOCK - 1)) // BLOCK * BLOCK).astype(F32)
    erow = lax.broadcasted_iota(I32, (lanes, lanes), 0)
    ecol = lax.broadcasted_iota(I32, (lanes, lanes), 1)
    together = erow // local_experts == ecol // local_experts
    prefix = jnp.where((erow < ecol) & together, 1.0, 0.0).astype(BF16)
    exact_off = jnp.dot(count8.astype(BF16), prefix, preferred_element_type=F32)[0:1]
    aligned_off = jnp.dot(padded8.astype(BF16), prefix, preferred_element_type=F32)[0:1]
    total = jnp.dot(count8.astype(BF16), jnp.where(together, 1.0, 0.0).astype(BF16), preferred_element_type=F32)[0:1]
    device = (lax.broadcasted_iota(I32, (1, lanes), 1) // local_experts * BASE).astype(F32)
    aligned_row = rank + (aligned_off + device) + 1.0
    exact_row = rank + (exact_off + device) + 1.0
    aligned = jnp.zeros((seq_len, lanes), F32)
    exact = jnp.zeros((seq_len, lanes), F32)
    for j in range(top_k):
        aligned += jnp.where(lane == j, jnp.sum(hits[j] * aligned_row, axis=1, keepdims=True), 0.0)
        exact += jnp.where(lane == j, jnp.sum(hits[j] * exact_row, axis=1, keepdims=True), 0.0)
    table_ref[0] = (jnp.transpose(aligned, (1, 0))[:8]).astype(I32) - 1
    table_ref[0, COUNT_ROW : COUNT_ROW + 1, :lanes] = count8[:1].astype(I32)
    table_ref[0, MOST_ROW : MOST_ROW + 1, :lanes] = jnp.broadcast_to(
        jnp.max(total, axis=1, keepdims=True), (1, lanes)
    ).astype(I32)
    exact_ref[0] = exact[:, :8].astype(I32) - 1


def route(experts, slots, local_experts, group):
    batches, seq_len, top_k = experts.shape
    return pl.pallas_call(
        functools.partial(route_kernel, local_experts, top_k),
        grid=(batches,),
        in_specs=[pl.BlockSpec((1, seq_len, top_k), lambda b: (b, 0, 0))] * 2,
        out_specs=[
            pl.BlockSpec((1, 8, seq_len), lambda b: (b, 0, 0)),
            pl.BlockSpec((1, seq_len, 8), lambda b: (b, 0, 0)),
        ],
        out_shape=[
            jax.ShapeDtypeStruct((batches, 8, seq_len), I32),
            jax.ShapeDtypeStruct((batches, seq_len, 8), I32),
        ],
        compiler_params=pltpu.CompilerParams(vmem_limit_bytes=VMEM_LIMIT // 2),
        cost_estimate=pl.CostEstimate(flops=10**9, bytes_accessed=10**6, transcendentals=0),
        name="route",
    )(experts, slots)


def front_kernel(
    group, top_k, head_dim,
    xa_ref, xb_ref, q_ref, k_ref, v_ref, wo_ref, mgain_ref, table_ref,
    ha_ref, hb_ref, ua_ref, ub_ref, tables_ref, xs_ref,
    qkv, wo, xbuf, acc, hbuf, ubuf, codes, urows, xrows,
    q_sem, w_sem, x_sem, h_sem, u_sem, t_sem, load_sem, put_sem, send_sem, recv_sem, tsend_sem, trecv_sem,
):
    seq_len, model_dim = xbuf.shape
    half = seq_len // 2
    pairs = wo.shape[0]
    scale = head_dim**-0.5
    chips = group // 2
    me = lax.axis_index("ep")
    chip, core = me // 2, lax.rem(me, 2)
    mate = chip * 2 + 1 - core
    left = lax.rem(chip + chips - 1, chips) * 2 + core
    right = lax.rem(chip + 1, chips) * 2 + core
    far = lax.rem(chip + 2, chips) * 2 + core

    def weight_copy(p):
        return pltpu.make_async_copy(wo_ref.at[p], wo.at[p], w_sem.at[p])

    def qkv_copies(b):
        rows = pl.ds(b * seq_len, seq_len)
        return [
            pltpu.make_async_copy(src.at[:, rows], qkv.at[b, i], q_sem.at[b, i])
            for i, src in enumerate((q_ref, k_ref, v_ref))
        ]

    load_a = pltpu.make_async_copy(xa_ref, xbuf, x_sem.at[0])
    load_b = pltpu.make_async_copy(xb_ref, xbuf, x_sem.at[1])
    load_a.start()
    for c in qkv_copies(0):
        c.start()

    def start_weights(p, _):
        weight_copy(p).start()
        return 0

    lax.fori_loop(0, pairs, start_weights, 0)

    barrier = pltpu.get_barrier_semaphore()
    for d in range(1, group):
        pl.semaphore_signal(barrier, inc=1, device_id={"ep": lax.rem(me + d, group)}, device_id_type=pl.DeviceIdType.MESH)
    pl.semaphore_wait(barrier, group - 1)

    def table_copy(d, slot):
        return pltpu.make_async_remote_copy(
            src_ref=table_ref, dst_ref=tables_ref.at[slot], send_sem=tsend_sem.at[d], recv_sem=trecv_sem.at[d],
            device_id={"ep": lax.rem(me + d, group)}, device_id_type=pl.DeviceIdType.MESH,
        )

    own_table = pltpu.make_async_copy(table_ref, tables_ref.at[me], t_sem.at[0])
    own_table.start()
    for d in range(1, group):
        table_copy(d, me).start()

    part0, part1, both = pl.ds(0, half), pl.ds(half, half), pl.ds(0, seq_len)

    def u_copy(k, whose, rows, to):
        return pltpu.make_async_remote_copy(
            src_ref=ua_ref.at[whose, rows], dst_ref=ua_ref.at[whose, rows], send_sem=send_sem.at[k],
            recv_sem=recv_sem.at[k], device_id={"ep": to}, device_id_type=pl.DeviceIdType.MESH,
        )

    def mate_of(device):
        return device // 2 * 2 + 1 - lax.rem(device, 2)

    sends = [
        (me, part0, right), (me, part1, right), (me, part1, left), (me, part0, left),
        (left, part0, right), (right, part1, left), (me, both, mate),
        (left, part0, mate), (left, part1, mate), (right, part1, mate), (right, part0, mate),
        (far, part0, mate), (far, part1, mate),
    ]
    received = [
        left, left, right, right, far, far, mate,
        mate_of(left), mate_of(left), mate_of(right), mate_of(right), mate_of(far), mate_of(far),
    ]

    def send(k):
        u_copy(k, *sends[k]).start()

    def arrived(k):
        u_copy(k, received[k], sends[k][1], sends[k][2]).wait_recv()

    def attend_head(q, k, v, first_row):
        scores = lax.dot_general(q, k, (((1,), (1,)), ((), ())), preferred_element_type=F32) * scale
        rows = lax.broadcasted_iota(I32, scores.shape, 0) + first_row
        cols = lax.broadcasted_iota(I32, scores.shape, 1)
        scores = jnp.where(rows >= cols, scores, MASK_VALUE)
        top = jnp.max(scores, axis=-1, keepdims=True)
        e = jnp.exp(scores - top)
        prob = (e / jnp.sum(e, axis=-1, keepdims=True)).astype(BF16)
        return jnp.dot(prob, v, preferred_element_type=F32).astype(BF16)

    def begin():
        for r in range(0, seq_len, 128):
            acc[r : r + 128] = xbuf[r : r + 128].astype(F32)

    def head_pair(b, p):
        low, high = [], []
        for i in range(2):
            q, k, v = (qkv.at[b, n, 2 * p + i] for n in range(3))
            low.append(attend_head(q[:half], k[:half], v[:half], 0))
            high.append(attend_head(q[half:], k[...], v[...], half))
        w = wo[p]
        acc[:half] += jnp.dot(jnp.concatenate(low, axis=1), w, preferred_element_type=F32)
        acc[half:] += jnp.dot(jnp.concatenate(high, axis=1), w, preferred_element_type=F32)

    def finish():
        gain = mgain_ref[...].astype(F32)
        for r in range(0, seq_len, 128):
            h = acc[r : r + 128].astype(BF16)
            hbuf[r : r + 128] = h
            ubuf[r : r + 128] = rms_rows(h.astype(F32), gain)

    load_a.wait()
    begin()
    load_b.start()
    for c in qkv_copies(0):
        c.wait()
    for c in qkv_copies(1):
        c.start()

    def pair_a(p, _):
        weight_copy(p).wait()
        head_pair(0, p)
        return 0

    lax.fori_loop(0, pairs, pair_a, 0)
    finish()
    put_u = pltpu.make_async_copy(ubuf, ua_ref.at[me], u_sem.at[0])
    put_h = pltpu.make_async_copy(hbuf, ha_ref, h_sem.at[0])
    put_u.start()
    put_h.start()
    put_u.wait()
    for k in (0, 2, 6, 1, 3):
        send(k)

    load_b.wait()
    begin()
    for c in qkv_copies(1):
        c.wait()

    def pair_b(p, _):
        head_pair(1, p)

        @pl.when(p == pairs - 1)
        def _():
            arrived(0)
            send(4)
            send(7)
            arrived(2)
            send(5)
            send(9)

        return 0

    lax.fori_loop(0, pairs, pair_b, 0)
    put_h.wait()
    finish()
    put_ub = pltpu.make_async_copy(ubuf, ub_ref, u_sem.at[1])
    put_hb = pltpu.make_async_copy(hbuf, hb_ref, h_sem.at[1])
    put_ub.start()
    put_hb.start()

    own_table.wait()
    for d in range(1, group):
        table_copy(d, lax.rem(me + group - d, group)).wait_recv()
    load_codes = pltpu.make_async_copy(tables_ref.at[:, 0], codes, t_sem.at[1])
    load_codes.start()
    load_codes.wait()
    chunk = xrows.shape[1]
    chunks = xs_ref.shape[1] // chunk

    def select(source):
        load = pltpu.make_async_copy(ua_ref.at[source], urows, load_sem)
        load.start()
        load.wait()
        code = codes[source] - me * BASE

        def pick_chunk(i, _):
            row = lax.broadcasted_iota(I32, (chunk, seq_len), 0) + i * chunk
            pick = jnp.zeros((chunk, seq_len), F32)
            for j in range(top_k):
                pick = jnp.where(row == code[j : j + 1, :], 1.0, pick)
            slot = lax.rem(i, 2)
            put = pltpu.make_async_copy(
                xrows.at[slot], xs_ref.at[source, pl.ds(pl.multiple_of(i * chunk, chunk), chunk)], put_sem.at[slot]
            )

            @pl.when(i >= 2)
            def _():
                put.wait()

            xrows[slot] = jnp.dot(pick.astype(BF16), urows[...], preferred_element_type=F32).astype(BF16)
            put.start()
            return 0

        lax.fori_loop(0, chunks, pick_chunk, 0)
        for slot in range(2):
            pltpu.make_async_copy(xrows.at[slot], xs_ref.at[source, pl.ds(0, chunk)], put_sem.at[slot]).wait()

    select(me)
    arrived(6)
    select(mate)
    arrived(1)
    send(8)
    arrived(3)
    send(10)
    select(left)
    select(right)
    arrived(7)
    arrived(8)
    select(mate_of(left))
    arrived(9)
    arrived(10)
    select(mate_of(right))
    arrived(4)
    send(11)
    arrived(5)
    send(12)
    select(far)
    arrived(11)
    arrived(12)
    select(mate_of(far))

    for k in range(len(sends)):
        u_copy(k, *sends[k]).wait_send()
    for d in range(1, group):
        table_copy(d, me).wait_send()
    put_ub.wait()
    put_hb.wait()


def front(xa, xb, w_query, w_key, w_value, w_out, attn_gain, moe_gain, table, group, top_k, full_rows):
    seq_len, model_dim = xa.shape
    heads, head_dim = w_query.shape[1:]
    pairs = heads // 2
    wide = 2 * head_dim
    x = jnp.concatenate([xa, xb], axis=0)
    normed = rms_rows(x.astype(F32), attn_gain.astype(F32))
    q, k, v = (
        jnp.einsum("td,dhe->hte", normed, w, preferred_element_type=F32).astype(BF16) for w in (w_query, w_key, w_value)
    )
    wo = w_out.reshape(pairs, wide, model_dim)
    rows = jax.ShapeDtypeStruct((seq_len, model_dim), BF16)
    anywhere = pl.BlockSpec(memory_space=pl.ANY)
    vmem = pl.BlockSpec(memory_space=pltpu.VMEM)
    dma = pltpu.SemaphoreType.DMA
    chunk = 256
    return pl.pallas_call(
        functools.partial(front_kernel, group, top_k, head_dim),
        in_specs=[anywhere] * 6 + [vmem] * 2,
        out_specs=[anywhere] * 6,
        out_shape=[
            rows,
            rows,
            jax.ShapeDtypeStruct((group, seq_len, model_dim), BF16),
            rows,
            jax.ShapeDtypeStruct((group,) + table.shape, I32),
            jax.ShapeDtypeStruct((group, full_rows, model_dim), BF16),
        ],
        scratch_shapes=[
            pltpu.VMEM((2, 3, heads, seq_len, head_dim), BF16),
            pltpu.VMEM((pairs, wide, model_dim), BF16),
            pltpu.VMEM((seq_len, model_dim), BF16),
            pltpu.VMEM((seq_len, model_dim), F32),
            pltpu.VMEM((seq_len, model_dim), BF16),
            pltpu.VMEM((seq_len, model_dim), BF16),
            pltpu.VMEM((group,) + table.shape[1:], I32),
            pltpu.VMEM((seq_len, model_dim), BF16),
            pltpu.VMEM((2, chunk, model_dim), BF16),
            dma((2, 3)),
            dma((pairs,)),
            dma((2,)),
            dma((2,)),
            dma((2,)),
            dma((2,)),
            dma,
            dma((2,)),
            dma((13,)),
            dma((13,)),
            dma((group,)),
            dma((group,)),
        ],
        compiler_params=pltpu.CompilerParams(vmem_limit_bytes=VMEM_LIMIT, collective_id=0, has_side_effects=True),
        cost_estimate=pl.CostEstimate(
            flops=2 * (8 * seq_len * model_dim * model_dim + 4 * seq_len * seq_len * model_dim),
            bytes_accessed=2 * 4 * model_dim * model_dim,
            transcendentals=2 * heads * seq_len * seq_len,
        ),
        name="front",
    )(xa, xb, q, k, v, wo, moe_gain.reshape(1, -1), table)


def select_kernel(top_k, me_ref, code_ref, u_ref, out_ref):
    aligned_rows, seq_len = out_ref.shape[1], u_ref.shape[1]
    code = code_ref[0, 0] - me_ref[0] * BASE
    chunk = 160 if aligned_rows % 160 == 0 else 256
    for first in range(0, aligned_rows, chunk):
        row = lax.broadcasted_iota(I32, (chunk, seq_len), 0) + first
        pick = jnp.zeros((chunk, seq_len), F32)
        for j in range(top_k):
            pick = jnp.where(row == code[j : j + 1, :], 1.0, pick)
        out_ref[0, first : first + chunk] = jnp.dot(pick.astype(BF16), u_ref[0], preferred_element_type=F32).astype(BF16)


def select_rows(me, tables, batch, u_all, aligned_rows, top_k):
    group, seq_len, model_dim = u_all.shape
    return pl.pallas_call(
        functools.partial(select_kernel, top_k),
        grid_spec=pltpu.PrefetchScalarGridSpec(
            num_scalar_prefetch=1,
            grid=(group,),
            in_specs=[
                pl.BlockSpec((1, 1, 8, seq_len), lambda i, me: (i, batch, 0, 0)),
                pl.BlockSpec((1, seq_len, model_dim), lambda i, me: (i, 0, 0)),
            ],
            out_specs=pl.BlockSpec((1, aligned_rows, model_dim), lambda i, me: (i, 0, 0)),
        ),
        out_shape=jax.ShapeDtypeStruct((group, aligned_rows, model_dim), BF16),
        compiler_params=pltpu.CompilerParams(vmem_limit_bytes=VMEM_LIMIT),
        cost_estimate=pl.CostEstimate(
            flops=2 * group * aligned_rows * seq_len * model_dim,
            bytes_accessed=2 * group * (aligned_rows + seq_len) * model_dim,
            transcendentals=0,
        ),
        name="select",
    )(me, tables, u_all)


def expert_kernel(me_ref, count_ref, x_in, gate_ref, up_ref, down_ref, x_out, buf, blocks_ref, offset_ref, in_sem, out_sem):
    step = pl.program_id(0)
    steps = pl.num_programs(0)
    places = x_in.shape[0]

    def each_block(expert, slot, fn):
        def per_place(place, filled):
            n = blocks_ref[place, expert]
            first = offset_ref[place, expert]

            def per_block(b, _):
                rows = pl.ds(pl.multiple_of(first + b * BLOCK, BLOCK), BLOCK)
                held = pl.ds(pl.multiple_of((filled + b) * BLOCK, BLOCK), BLOCK)
                fn(place, rows, buf.at[slot, held])
                return 0

            lax.fori_loop(0, n, per_block, 0)
            return filled + n

        return lax.fori_loop(0, places, per_place, jnp.int32(0))

    def fetch(place, rows, held, slot):
        pltpu.make_async_copy(x_in.at[place, rows], held, in_sem.at[slot]).start()

    def put(place, rows, held, slot):
        pltpu.make_async_copy(held, x_out.at[place, rows], out_sem.at[slot]).start()

    def fetched(place, rows, held, slot):
        pltpu.make_async_copy(x_in.at[place, rows], held, in_sem.at[slot]).wait()

    def gone(place, rows, held, slot):
        pltpu.make_async_copy(held, x_out.at[place, rows], out_sem.at[slot]).wait()

    def over(expert, fn):
        slot = lax.rem(expert, 3)
        return each_block(expert, slot, functools.partial(fn, slot=slot))

    @pl.when(step == 0)
    def _():
        def plan(place, _):
            def one(e, filled):
                n = (count_ref[place, me_ref[0] * steps + e] + (BLOCK - 1)) // BLOCK
                blocks_ref[place, e] = n
                offset_ref[place, e] = filled * BLOCK
                return filled + n

            lax.fori_loop(0, steps, one, jnp.int32(0))
            return 0

        lax.fori_loop(0, places, plan, 0)
        over(step, fetch)

    @pl.when(step >= 2)
    def _():
        over(step - 2, gone)

    @pl.when(step + 1 < steps)
    def _():
        over(step + 1, fetch)

    filled = over(step, fetched)
    slot = lax.rem(step, 3)

    def tile(i, _):
        rows = pl.ds(pl.multiple_of(i * TILE, TILE), TILE)
        x = buf[slot, rows]
        gate = jnp.dot(x, gate_ref[0], preferred_element_type=F32)
        up = jnp.dot(x, up_ref[0], preferred_element_type=F32)
        hidden = (gate * jax.nn.sigmoid(gate) * up).astype(BF16)
        buf[slot, rows] = jnp.dot(hidden, down_ref[0], preferred_element_type=F32).astype(BF16)
        return 0

    lax.fori_loop(0, (filled * BLOCK + TILE - 1) // TILE, tile, 0)
    over(step, put)

    @pl.when(step + 1 == steps)
    def _():
        over(step - 1, gone)
        over(step, gone)


def expert_ffn(me, counts, x, w_gate, w_up, w_down, capacity):
    places, aligned_rows, model_dim = x.shape
    experts, _, hidden_dim = w_gate.shape
    held = -(-places * capacity // TILE) * TILE
    weight_in = pl.BlockSpec((1, model_dim, hidden_dim), lambda e, b, o: (e, 0, 0))
    return pl.pallas_call(
        expert_kernel,
        grid_spec=pltpu.PrefetchScalarGridSpec(
            num_scalar_prefetch=2,
            grid=(experts,),
            in_specs=[
                pl.BlockSpec(memory_space=pl.ANY),
                weight_in,
                weight_in,
                pl.BlockSpec((1, hidden_dim, model_dim), lambda e, b, o: (e, 0, 0)),
            ],
            out_specs=pl.BlockSpec(memory_space=pl.ANY),
            scratch_shapes=[
                pltpu.VMEM((3, held, model_dim), BF16),
                pltpu.SMEM((places, experts), I32),
                pltpu.SMEM((places, experts), I32),
                pltpu.SemaphoreType.DMA((3,)),
                pltpu.SemaphoreType.DMA((3,)),
            ],
        ),
        out_shape=jax.ShapeDtypeStruct(x.shape, BF16),
        input_output_aliases={2: 0},
        compiler_params=pltpu.CompilerParams(vmem_limit_bytes=VMEM_LIMIT),
        cost_estimate=pl.CostEstimate(
            flops=6 * 3072 * model_dim * hidden_dim,
            bytes_accessed=6 * experts * model_dim * hidden_dim,
            transcendentals=0,
        ),
        name="experts",
    )(me, counts, x, w_gate, w_up, w_down)


def pack_kernel(local_experts, me_ref, count_ref, x_ref, out_ref):
    rows_out, aligned_rows = out_ref.shape[1], x_ref.shape[1]
    place = pl.program_id(0)
    chunk = 176 if rows_out % 176 == 0 else 256
    for first in range(0, rows_out, chunk):
        row = lax.broadcasted_iota(I32, (chunk, 1), 0) + first
        source = jnp.full((chunk, 1), -1, I32)
        off, aligned_off = jnp.int32(0), jnp.int32(0)
        for e in range(local_experts):
            n = count_ref[place, me_ref[0] * local_experts + e]
            inside = (row >= off) & (row < off + n)
            source = jnp.where(inside, row + (aligned_off - off), source)
            off = off + n
            aligned_off = aligned_off + (n + (BLOCK - 1)) // BLOCK * BLOCK
        col = lax.broadcasted_iota(I32, (chunk, aligned_rows), 1)
        pick = jnp.where(col == source, 1.0, 0.0).astype(BF16)
        out_ref[0, first : first + chunk] = jnp.dot(pick, x_ref[0], preferred_element_type=F32).astype(BF16)


def pack_rows(me, counts, x, local_experts, aligned_rows, rows_out):
    places, _, model_dim = x.shape
    return pl.pallas_call(
        functools.partial(pack_kernel, local_experts),
        grid_spec=pltpu.PrefetchScalarGridSpec(
            num_scalar_prefetch=2,
            grid=(places,),
            in_specs=[pl.BlockSpec((1, aligned_rows, model_dim), lambda i, m, c: (i, 0, 0))],
            out_specs=pl.BlockSpec((1, rows_out, model_dim), lambda i, m, c: (i, 0, 0)),
        ),
        out_shape=jax.ShapeDtypeStruct((places, rows_out, model_dim), BF16),
        compiler_params=pltpu.CompilerParams(vmem_limit_bytes=VMEM_LIMIT),
        cost_estimate=pl.CostEstimate(
            flops=2 * places * aligned_rows * rows_out * model_dim,
            bytes_accessed=2 * places * (aligned_rows + rows_out) * model_dim,
            transcendentals=0,
        ),
        name="pack",
    )(me, counts, x)


def combine_kernel(top_k, code_ref, gates_ref, recv_ref, h_ref, out_ref, acc_ref):
    step = pl.program_id(0)
    rows = recv_ref.shape[0]

    @pl.when(step == 0)
    def _():
        acc_ref[...] = h_ref[...].astype(F32)

    code = code_ref[...]
    gates = gates_ref[...]
    col = lax.broadcasted_iota(I32, (code.shape[0], rows), 1) + step * rows
    mix = jnp.zeros(col.shape, F32)
    for j in range(top_k):
        mix = jnp.where(col == code[:, j : j + 1], gates[:, j : j + 1], mix)
    acc_ref[...] += jnp.dot(mix.astype(BF16), recv_ref[...], preferred_element_type=F32)

    @pl.when(step == pl.num_programs(0) - 1)
    def _():
        out_ref[...] = acc_ref[...].astype(BF16)


def combine(residual, recv, code, gates):
    seq_len, model_dim = residual.shape
    group, rows, _ = recv.shape
    top_k = gates.shape[1]
    column = jnp.where(code >= 0, code // BASE * rows + code % BASE, -1)
    gates_f = jnp.pad(gates.astype(F32), ((0, 0), (0, 8 - top_k)))
    rows_step = 256
    whole = lambda r, c: pl.BlockSpec((r, c), lambda i: (0, 0))
    return pl.pallas_call(
        functools.partial(combine_kernel, top_k),
        grid=(group * rows // rows_step,),
        in_specs=[
            whole(seq_len, 8),
            whole(seq_len, 8),
            pl.BlockSpec((rows_step, model_dim), lambda i: (i, 0)),
            whole(seq_len, model_dim),
        ],
        out_specs=whole(seq_len, model_dim),
        out_shape=jax.ShapeDtypeStruct((seq_len, model_dim), BF16),
        scratch_shapes=[pltpu.VMEM((seq_len, model_dim), F32)],
        compiler_params=pltpu.CompilerParams(vmem_limit_bytes=VMEM_LIMIT),
        cost_estimate=pl.CostEstimate(
            flops=2 * seq_len * group * rows * model_dim,
            bytes_accessed=2 * (group * rows + 2 * seq_len) * model_dim,
            transcendentals=0,
        ),
        name="combine",
    )(column, gates_f, recv.reshape(group * rows, model_dim), residual)


def capacity_of(seq_len, top_k, experts_total):
    return 8 * max(1, (seq_len * top_k) // (4 * experts_total))


def solution(mesh):
    group = mesh.shape["ep"]
    row_spec = P(("dp", "ep"), None)
    full_spec = P(None, None, None)
    gain_spec = P(None)
    expert_spec = P("ep", None, None)
    in_specs = (row_spec,) * 8 + (gain_spec, full_spec, full_spec, full_spec, full_spec, gain_spec) + (expert_spec,) * 3

    def device_fn(
        tokens_a, experts_a, slots_a, gates_a, tokens_b, experts_b, slots_b, gates_b,
        attn_gain, w_query, w_key, w_value, w_out, moe_gain, w_gate, w_up, w_down,
    ):
        seq_len, model_dim = tokens_a.shape
        local_experts = w_gate.shape[0]
        capacity = capacity_of(seq_len, experts_a.shape[1], local_experts * group)
        full_rows = local_experts * capacity
        me = lax.axis_index("ep").astype(I32)

        top_k = experts_a.shape[1]
        me1 = me.reshape(1)
        table, exact = route(jnp.stack([experts_a, experts_b]), jnp.stack([slots_a, slots_b]), local_experts, group)
        h_a, h_b, _, u_b, tables, x_a = front(
            tokens_a, tokens_b, w_query, w_key, w_value, w_out, attn_gain, moe_gain, table, group, top_k, full_rows
        )
        counts = tables[:, :, COUNT_ROW, : local_experts * group]
        largest = jnp.max(tables[:, :, MOST_ROW, 0])

        def moe(rows_out, aligned_rows, operands):
            x_a, u_b, h_a, h_b, tables, counts = operands

            def experts_side(b, x):
                o = expert_ffn(me1, counts[:, b], x, w_gate, w_up, w_down, capacity)
                packed = pack_rows(me1, counts[:, b], o, local_experts, aligned_rows, rows_out)
                return lax.all_to_all(packed, "ep", 0, 0, tiled=True)

            u_all = lax.all_gather(u_b, "ep", axis=0, tiled=False)
            back_a = experts_side(0, x_a)
            back_b = experts_side(1, select_rows(me1, tables, 1, u_all, aligned_rows, top_k))
            return combine(h_a, back_a, exact[0], gates_a), combine(h_b, back_b, exact[1], gates_b)

        sizes = [r for r in (352,) if r < full_rows] + [full_rows]
        branches = []
        for r in sizes:
            aligned_rows = min(full_rows, -(-(r + local_experts * (BLOCK - 1)) // 160) * 160)
            branches.append(functools.partial(moe, r, aligned_rows))
        which = jnp.int32(0)
        for r in sizes[:-1]:
            which = which + (largest > r).astype(I32)
        return lax.switch(which, branches, (x_a, u_b, h_a, h_b, tables, counts))

    return jax.shard_map(device_fn, mesh=mesh, in_specs=in_specs, out_specs=(row_spec, row_spec), check_vma=False)
```

time: 1440 us -> 573 us (0.40)
  waiting for transfers between devices: 599 us -> 120 us
  matrix products: 421 us -> 35.9 us
  Pallas kernels: 0 us -> 365 us
  local copies, waits for them, and re-layouts: 267 us -> 2.88 us
  other arithmetic: 116 us -> 7.7 us
  starting transfers between devices: 28 us -> 11.2 us
    all_to_all x4 -> x2, waiting for transfers between devices: 599 us -> 119 us  [experts_side(): return lax.all_to_all(packed, 'ep', 0, 0, tiled=True)]
    dot_general x16 -> x3, matrix products: 421 us -> 35.9 us  [front(): jnp.einsum('td,dhe->hte', normed, w, preferred_element_type=F32)]
    pallas_call x0 -> x9, Pallas kernels: none -> 365 us  [the longest x2 164 us: expert_ffn(): pl.pallas_call(expert_kernel, grid_spec=pltpu.PrefetchScalarGridSpec(num_...]
    gather x4 -> x0, local copies, waits for them, and re-layouts: 149 us -> none  [the longest x2 79 us: dispatch_rows(): jnp.take(normed, source, axis=0, mode='fill', fill_value=0)]
    select_n x9 -> x1, other arithmetic: 65.4 us -> 1.3 us  [combine(): column = jnp.where(code >= 0, code // BASE * rows + code % BASE, -1)]
    convert_element_type x2 -> x0, local copies, waits for them, and re-layouts: 42.1 us -> none  [expert_ffn(): jnp.einsum('pecf,efd->pecd', hidden, w_down, preferred_element_type=jnp.f...]
    reshape x6 -> x1, local copies, waits for them, and re-layouts: 41.4 us -> 0.6 us  [front(): moe_gain.reshape(1, -1)]
    sub x2 -> x0, other arithmetic: 36.2 us -> none  [attention_block(): attn_prob = jax.nn.softmax(scores, axis=-1).astype(jnp.bfloat16)]
  transfers between devices with their start and end apart: 4 -> 3, of which waited for: 4 -> 2; matrix products, arithmetic and copies ran while one was open for 35% -> 1% of each run, Pallas kernels for 0% -> 41%
where the time goes in v1:
time: 573 us; the launch traced here: 566 us
  Pallas kernels  365 us (64%)
  waiting for transfers between devices  120 us (21%)
  matrix products  35.9 us (6%)
  between operations  15.5 us (3%)
  starting transfers between devices  11.2 us (2%)
  loops' own time  7.81 us (1%)
  other arithmetic  7.7 us (1%)
    pallas_call x2, Pallas kernels, expert_ffn(): pl.pallas_call(expert_kernel, grid_spec=pltpu.PrefetchScalarGridSpec(num_...  164 us
    all_to_all x2, waiting for transfers between devices, experts_side(): return lax.all_to_all(packed, 'ep', 0, 0, tiled=True)  119 us
    pallas_call x1, Pallas kernels, front(): pl.pallas_call(functools.partial(front_kernel, group, top_k, head_dim), i...  109 us
    pallas_call x2, Pallas kernels, combine(): pl.pallas_call(functools.partial(combine_kernel, top_k), grid=(group * ro...  38.3 us
    dot_general x3, matrix products, front(): jnp.einsum('td,dhe->hte', normed, w, preferred_element_type=F32)  35.9 us
    pallas_call x2, Pallas kernels, pack_rows(): pl.pallas_call(functools.partial(pack_kernel, local_experts), grid_spec=p...  31.5 us
    pallas_call x1, Pallas kernels, select_rows(): pl.pallas_call(functools.partial(select_kernel, top_k), grid_spec=pltpu.P...  17.3 us
  transfers between devices with their start and end apart: 3, of which 2 were waited for; matrix products, arithmetic and copies ran while one was open for 1% of the time, Pallas kernels for 41%

profile of v1, /device:TPU:112, one launch (start us, length us, event | category | flops | bytes accessed | tf_op | source)
XLA Modules:
  0.0 565.6 jit_solution(5422393937386997545)
XLA Ops:
  7.2 0.0 slice-start
  7.2 0.0 slice-start.2
  7.2 2.8 fusion.32
  10.0 1.4 convert_element_type.37
  11.5 14.1 %convert_bitcast_fusion.v_ref = bf16[16,1024,128]{2,1,0:T(8,128)(2,1)} fusion(bf16[2048,16,128]{2,1,0:T(8,128)(2,1)} %param.30, f32[2048]{0:T(1024)S(1)} %convert_element_type.37, f32[1024]{0:T(1024)S(1)} %add_rsqrt_fusion, bf16[512,2048]{1,0:T(8,128)(2,1)} %xb_ref.1, bf16[512,2048]{1,0:T(8,128)(2,1)} %xa_ref.1), kind=kOutput, calls=%fused_computation.87 | convolution fusion | flops 8606711808 | bytes 16789504 | tf_op jit(solution)/shard_map/td,dhe->hte/dot_general | solution.py:328
  25.6 0.0 slice-done
  25.6 0.0 copy-done.1
  25.6 0.0 copy-done.2
  25.6 0.0 slice-done.1
  25.6 10.8 %convert_bitcast_fusion.1.k_ref = bf16[16,1024,128]{2,1,0:T(8,128)(2,1)} fusion(bf16[2048,16,128]{2,1,0:T(8,128)(2,1)S(1)} %bitcast.135, f32[2048]{0:T(1024)S(1)} %convert_element_type.37, f32[1024]{0:T(1024)S(1)} %add_rsqrt_fusion, bf16[512,2048]{1,0:T(8,128)(2,1)S(1)} %copy-done.2, bf16[512,2048]{1,0:T(8,128)(2,1)S(1)} %copy-done.1), kind=kOutput, calls=%fused_computation.88 | convolution fusion | flops 8606711808 | bytes 16789504 | tf_op jit(solution)/shard_map/td,dhe->hte/dot_general | solution.py:328
  36.5 0.0 slice-done.2
  36.5 0.0 slice-done.3
  36.5 0.0 copy-start.10
  36.5 0.0 copy-start.11
  36.5 0.0 copy-start.12
  36.5 0.0 copy-start.13
  36.5 11.0 %convert_bitcast_fusion.2.q_ref = bf16[16,1024,128]{2,1,0:T(8,128)(2,1)} fusion(bf16[2048,16,128]{2,1,0:T(8,128)(2,1)S(1)} %bitcast.137, f32[2048]{0:T(1024)S(1)} %convert_element_type.37, f32[1024]{0:T(1024)S(1)} %add_rsqrt_fusion, bf16[512,2048]{1,0:T(8,128)(2,1)S(1)} %copy-done.2, bf16[512,2048]{1,0:T(8,128)(2,1)S(1)} %copy-done.1), kind=kOutput, calls=%fused_computation.89 | convolution fusion | flops 8606711808 | bytes 16789504 | tf_op jit(solution)/shard_map/td,dhe->hte/dot_general | solution.py:328
  47.5 0.0 copy-done.9
  47.6 0.2 copy.53.experts_ref
  47.9 0.2 copy.54.slots_ref
  48.1 5.0 route.1
  53.1 0.6 copy-done
  53.8 0.6 reshape.35.mgain_ref
  54.4 109.1 %front.1 = (bf16[512,2048]{1,0:T(8,128)(2,1)}, bf16[512,2048]{1,0:T(8,128)(2,1)}, bf16[8,512,2048]{2,1,0:T(8,128)(2,1)}, bf16[512,2048]{1,0:T(8,128)(2,1)}, s32[...) custom-call(bf16[512,2048]{1,0:T(8,128)(2,1)} %xa_ref.1, bf16[512,2048]{1,0:T(8,128)(2,1)} %xb_ref.1, ...), custom_call_target="tpu_custom_call" | custom-call | flops 38654705664 | bytes 33554432 | tf_op jit(solution)/shard_map/front/pallas_call | solution.py:336
  163.5 0.7 slice_reduce_fusion
  164.8 393.4 %conditional.1 = (bf16[512,2048]{1,0:T(8,128)(2,1)}, bf16[512,2048]{1,0:T(8,128)(2,1)}) conditional(s32[]{:T(128)} %clamp.3, (s32[2,512,8]{2,1,0:T(8,128)}, bf16[512,6]{0,1:T(8,128)(2,1)}, s32[8,2,8,512]{3,2,1,0:T(8,128)S(1)}, s32[]{:T(128)}, bf16[8,768,2048]{2,1,0:T(8,128)(2,1)}, /*index=5*/bf16[8,2048,1408]{2,1,0:T(8,128)(2,1)}, ...), branch_computations={%region_2.3_spmd, %region_3.4_spmd} | conditional | flops 183610048512 | bytes 686625024 | solution.py:678
  164.8 0.1 all-gather.5.cloned.1.call-start
  164.8 0.7 all-gather.5.cloned.1.call-update
  165.6 0.2 copy.56
  165.7 0.6 slice_bitcast_fusion.1
  166.3 81.9 %experts.4.x_ref = bf16[8,768,2048]{2,1,0:T(8,128)(2,1)} custom-call(s32[1]{0:T(128)} %bitcast.1.me_ref, s32[8,64]{1,0:T(8,128)} %get-tuple-element.177.count_ref, bf16[8,768,2048]{2,1,0:T(8,128)(2,1)} %get-tuple-element.56.x_in, bf16[8,2048,1408]{2,1,0:T(8,128)(2,1)} %get-tuple-element.114.gate_ref, ...), custom_call_target="tpu_custom_call", output_to_operand_aliasing={{}: (2, {})} | custom-call | flops 53150220288 | bytes 138412032 | tf_op jit(solution)/shard_map/cond/branch_0_fun/experts/pallas_call | solution.py:503
  248.2 15.7 %pack.4 = bf16[8,352,2048]{2,1,0:T(8,128)(2,1)} custom-call(s32[1]{0:T(128)} %bitcast.1.me_ref, s32[8,64]{1,0:T(8,128)} %get-tuple-element.177.count_ref, bf16[8,768,2048]{2,1,0:T(8,128)(2,1)} %experts.4.x_ref), custom_call_target="tpu_custom_call" | custom-call | flops 5536481280 | bytes 27262976 | tf_op jit(solution)/shard_map/cond/branch_0_fun/pack/pallas_call | solution.py:556
  264.0 5.4 all-to-all-start
  269.4 0.0 all-gather.5.cloned.1.call-done
  269.4 17.3 %select.30.x_in = bf16[8,480,2048]{2,1,0:T(8,128)(2,1)} custom-call(s32[1]{0:T(128)} %bitcast.1.me_ref, s32[8,2,8,512]{3,2,1,0:T(8,128)S(1)} %get-tuple-element.62.code_ref, bf16[8,512,2048]{2,1,0:T(8,128)(2,1)} %bitcast.132), custom_call_target="tpu_custom_call" | custom-call | flops 8053063680 | bytes 32505856 | tf_op jit(solution)/shard_map/cond/branch_0_fun/select/pallas_call | solution.py:395
  286.7 81.8 %experts.5.x_ref = bf16[8,480,2048]{2,1,0:T(8,128)(2,1)} custom-call(s32[1]{0:T(128)} %bitcast.1.me_ref, s32[8,64]{1,0:T(8,128)} %get-tuple-element.176.count_ref, bf16[8,480,2048]{2,1,0:T(8,128)(2,1)} %select.30.x_in, bf16[8,2048,1408]{2,1,0:T(8,128)(2,1)} %get-tuple-element.114.gate_ref, ...), custom_call_target="tpu_custom_call", output_to_operand_aliasing={{}: (2, {})} | custom-call | flops 53150220288 | bytes 138412032 | tf_op jit(solution)/shard_map/cond/branch_0_fun/experts/pallas_call | solution.py:503
  368.5 15.7 %pack.5 = bf16[8,352,2048]{2,1,0:T(8,128)(2,1)} custom-call(s32[1]{0:T(128)} %bitcast.1.me_ref, s32[8,64]{1,0:T(8,128)} %get-tuple-element.176.count_ref, bf16[8,480,2048]{2,1,0:T(8,128)(2,1)} %experts.5.x_ref), custom_call_target="tpu_custom_call" | custom-call | flops 5536481280 | bytes 27262976 | tf_op jit(solution)/shard_map/cond/branch_0_fun/pack/pallas_call | solution.py:556
  384.3 13.2 %all-to-all-done = bf16[8,352,2048]{2,1,0:T(8,128)(2,1)} async-done(((bf16[8,352,2048]{2,1,0:T(8,128)(2,1)}), bf16[8,352,2048]{2,1,0:T(8,128)(2,1)}, u32[]{:S(2)}, u32[]{:S(2)}) %all-to-all-start) | async-done | bytes 11534368 | tf_op jit(solution)/shard_map/cond/branch_0_fun/all_to_all | solution.py:663
  397.5 5.7 %all-to-all-start.1 = ((bf16[8,352,2048]{2,1,0:T(8,128)(2,1)}), bf16[8,352,2048]{2,1,0:T(8,128)(2,1)}, u32[]{:S(2)}, u32[]{:S(2)}) async-start(bf16[8,352,2048]{2,1,0:T(8,128)(2,1)} %pack.5), calls=%async_computation.1 | async-start | bytes 23068672 | tf_op jit(solution)/shard_map/cond/branch_0_fun/all_to_all | solution.py:663
  403.2 0.2 copy.57
  403.4 0.2 copy.55
  403.6 0.7 pad_convert_fusion.gates_ref
  404.3 0.7 pad_convert_fusion.1.gates_ref
  405.0 0.0 copy-done.3
  405.0 1.3 fusion.5
  406.3 19.1 %combine.4 = bf16[512,2048]{1,0:T(8,128)(2,1)} custom-call(s32[512,8]{1,0:T(8,128)} %get-tuple-element.175.code_ref, f32[512,8]{1,0:T(8,128)} %pad_convert_fusion.1.gates_ref, bf16[2816,2048]{1,0:T(8,128)(2,1)} %bitcast.4.recv_ref, bf16[512,2048]{1,0:T(8,128)(2,1)} %get-tuple-element.60.h_ref), custom_call_target="tpu_custom_call" | custom-call | flops 5905580032 | bytes 15728640 | tf_op jit(solution)/shard_map/cond/branch_0_fun/combine/pallas_call | solution.py:604
  425.5 105.8 %all-to-all-done.1 = bf16[8,352,2048]{2,1,0:T(8,128)(2,1)} async-done(((bf16[8,352,2048]{2,1,0:T(8,128)(2,1)}), bf16[8,352,2048]{2,1,0:T(8,128)(2,1)}, u32[]{:S(2)}, u32[]{:S(2)}) %all-to-all-start.1) | async-done | bytes 11534368 | tf_op jit(solution)/shard_map/cond/branch_0_fun/all_to_all | solution.py:663
  531.3 19.1 %combine.5 = bf16[512,2048]{1,0:T(8,128)(2,1)} custom-call(s32[512,8]{1,0:T(8,128)} %get-tuple-element.174.code_ref, f32[512,8]{1,0:T(8,128)} %pad_convert_fusion.gates_ref, bf16[2816,2048]{1,0:T(8,128)(2,1)} %bitcast.8.recv_ref, bf16[512,2048]{1,0:T(8,128)(2,1)} %get-tuple-element.64.h_ref), custom_call_target="tpu_custom_call" | custom-call | flops 5905580032 | bytes 15728640 | tf_op jit(solution)/shard_map/cond/branch_0_fun/combine/pallas_call | solution.py:604
  (25 shorter events, 0.1 us)
Async XLA Ops:
  7.2 18.4 %slice-start = ((s8[8388608]{0:T(1024)(128)(4,1)}), s8[4194304]{0:T(1024)(128)(4,1)S(1)}, s32[]{:S(2)}) async-start(s8[8388608]{0:T(1024)(128)(4,1)} %bitcast.134), calls=%async_computation.6 | async-start | bytes 8388608
  7.2 29.3 %slice-start.2 = ((s8[8388608]{0:T(1024)(128)(4,1)}), s8[4194304]{0:T(1024)(128)(4,1)S(1)}, s32[]{:S(2)}) async-start(s8[8388608]{0:T(1024)(128)(4,1)} %bitcast.136), calls=%async_computation.8 | async-start | bytes 8388608
  11.5 14.1 %copy-start.1 = (bf16[512,2048]{1,0:T(8,128)(2,1)S(1)}, bf16[512,2048]{1,0:T(8,128)(2,1)}, u32[]{:S(2)}) copy-start(bf16[512,2048]{1,0:T(8,128)(2,1)} %xa_ref.1) | copy-start | bytes 6291460
  11.5 14.1 %copy-start.2 = (bf16[512,2048]{1,0:T(8,128)(2,1)S(1)}, bf16[512,2048]{1,0:T(8,128)(2,1)}, u32[]{:S(2)}) copy-start(bf16[512,2048]{1,0:T(8,128)(2,1)} %xb_ref.1) | copy-start | bytes 6291460
  11.5 14.1 %slice-start.1 = ((s8[8388608]{0:T(1024)(128)(4,1)}), s8[4194304]{0:T(1024)(128)(4,1)S(1)}, s32[]{:S(2)}) async-start(s8[8388608]{0:T(1024)(128)(4,1)} %bitcast.134), calls=%async_computation.7 | async-start | bytes 8388608
  11.5 25.0 %slice-start.3 = ((s8[8388608]{0:T(1024)(128)(4,1)}), s8[4194304]{0:T(1024)(128)(4,1)S(1)}, s32[]{:S(2)}) async-start(s8[8388608]{0:T(1024)(128)(4,1)} %bitcast.136), calls=%async_computation.9 | async-start | bytes 8388608
  36.5 11.0 %copy-start.9 = (s32[512,6]{0,1:T(8,128)S(1)}, s32[512,6]{0,1:T(8,128)}, u32[]{:S(2)}) copy-start(s32[512,6]{0,1:T(8,128)} %param.20) | copy-start | bytes 36868
  36.5 11.0 %copy-start.10 = (s32[512,6]{0,1:T(8,128)S(1)}, s32[512,6]{0,1:T(8,128)}, u32[]{:S(2)}) copy-start(s32[512,6]{0,1:T(8,128)} %param.24) | copy-start | bytes 36868
  36.5 11.3 %copy-start.11 = (s32[512,6]{0,1:T(8,128)S(1)}, s32[512,6]{0,1:T(8,128)}, u32[]{:S(2)}) copy-start(s32[512,6]{0,1:T(8,128)} %param.21) | copy-start | bytes 36868
  36.5 11.3 %copy-start.12 = (s32[512,6]{0,1:T(8,128)S(1)}, s32[512,6]{0,1:T(8,128)}, u32[]{:S(2)}) copy-start(s32[512,6]{0,1:T(8,128)} %param.25) | copy-start | bytes 36868
  36.5 17.3 %copy-start.13 = (bf16[2048]{0:T(1024)(128)(2,1)S(1)}, bf16[2048]{0:T(1024)(128)(2,1)}, u32[]{:S(2)}) copy-start(bf16[2048]{0:T(1024)(128)(2,1)} %param.32) | copy-start | bytes 12292
  53.1 0.6 copy-start
  164.8 104.7 %all-gather.5.cloned.1.call-start = ((), (), s32[]{:S(2)}) async-start(), calls=%async_computation.4 | async-start | bytes 18874368 | tf_op jit(solution)/shard_map/cond/branch_0_fun/all_gather | solution.py:665
  264.0 133.5 %all-to-all-start = ((bf16[8,352,2048]{2,1,0:T(8,128)(2,1)}), bf16[8,352,2048]{2,1,0:T(8,128)(2,1)}, u32[]{:S(2)}, u32[]{:S(2)}) async-start(bf16[8,352,2048]{2,1,0:T(8,128)(2,1)} %pack.4), calls=%async_computation | async-start | bytes 23068672 | tf_op jit(solution)/shard_map/cond/branch_0_fun/all_to_all | solution.py:663
  384.3 18.9 %copy-start.7 = (bf16[512,6]{0,1:T(8,128)(2,1)S(1)}, bf16[512,6]{0,1:T(8,128)(2,1)}, u32[]{:S(2)}) copy-start(bf16[512,6]{0,1:T(8,128)(2,1)} %get-tuple-element.157) | copy-start | bytes 18436 | tf_op jit(solution)/shard_map/cond
  384.3 19.1 %copy-start.5 = (bf16[512,6]{0,1:T(8,128)(2,1)S(1)}, bf16[512,6]{0,1:T(8,128)(2,1)}, u32[]{:S(2)}) copy-start(bf16[512,6]{0,1:T(8,128)(2,1)} %get-tuple-element.149) | copy-start | bytes 18436 | tf_op jit(solution)/shard_map/cond
  384.3 20.8 %copy-start.3 = (s32[2,512,8]{2,1,0:T(8,128)S(1)}, s32[2,512,8]{2,1,0:T(8,128)}, u32[]{:S(2)}) copy-start(s32[2,512,8]{2,1,0:T(8,128)} %get-tuple-element.52) | copy-start | bytes 98308 | tf_op jit(solution)/shard_map/cond
  397.5 133.8 %all-to-all-start.1 = ((bf16[8,352,2048]{2,1,0:T(8,128)(2,1)}), bf16[8,352,2048]{2,1,0:T(8,128)(2,1)}, u32[]{:S(2)}, u32[]{:S(2)}) async-start(bf16[8,352,2048]{2,1,0:T(8,128)(2,1)} %pack.5), calls=%async_computation.1 | async-start | bytes 23068672 | tf_op jit(solution)/shard_map/cond/branch_0_fun/all_to_all | solution.py:663
Sparse Core Ops, SparseCore 0:
  167.2 81.3 all-gather.4

commit v2 on v1

v2 whole, which is shorter than its diff:
```python
import functools

import jax
import jax.numpy as jnp
from jax import lax
from jax.experimental import pallas as pl
from jax.experimental.pallas import tpu as pltpu
from jax.sharding import PartitionSpec as P

NORM_EPS = 1e-6
MASK_VALUE = -1e30
BLOCK = 16
TILE = 256
COUNT_ROW = 6
MOST_ROW = 7
BASE = 1024
VMEM_LIMIT = 65011712
F32 = jnp.float32
BF16 = jnp.bfloat16
I32 = jnp.int32
NONE = 0
SMALL = pl.CostEstimate(flops=1000000, bytes_accessed=1000000, transcendentals=NONE)


def at_origin(i):
    return (0, 0)


def by_place(i, *_):
    return (i, 0, 0)


def pieces(last, first=0):
    return [slice(r, r + 128) for r in range(first, last, 128)]


def repeat(times, body):
    lax.fori_loop(0, times, body, 0)


def row_ids(shape):
    return lax.broadcasted_iota(I32, shape, 0)


def col_ids(shape):
    return lax.broadcasted_iota(I32, shape, 1)


def rms_rows(rows_f, gain_f):
    inv_rms = lax.rsqrt(jnp.mean(rows_f * rows_f, axis=-1, keepdims=True) + NORM_EPS)
    return (rows_f * inv_rms * gain_f).astype(BF16)


def route_kernel(local_experts, top_k, experts_ref, slots_ref, table_ref, exact_ref):
    seq_len = experts_ref.shape[1]
    lanes = 128
    ids = experts_ref[0]
    slot = slots_ref[0]
    lane = col_ids((seq_len, lanes))
    hits = [jnp.where((ids[:, j : j + 1] == lane) & (slot[:, j : j + 1] >= 0), 1.0, 0.0) for j in range(top_k)]
    kept = functools.reduce(lambda a, b: a + b, hits)
    row = row_ids((seq_len, seq_len))
    col = col_ids((seq_len, seq_len))
    before = jnp.where(col < row, 1.0, 0.0).astype(BF16)
    rank = jnp.dot(before, kept.astype(BF16), preferred_element_type=F32)
    count8 = jnp.broadcast_to(jnp.sum(kept, axis=0, keepdims=True), (8, lanes))
    padded8 = ((count8.astype(I32) + (BLOCK - 1)) // BLOCK * BLOCK).astype(F32)
    erow = row_ids((lanes, lanes))
    ecol = col_ids((lanes, lanes))
    together = erow // local_experts == ecol // local_experts
    prefix = jnp.where((erow < ecol) & together, 1.0, 0.0).astype(BF16)
    exact_off = jnp.dot(count8.astype(BF16), prefix, preferred_element_type=F32)[0:1]
    aligned_off = jnp.dot(padded8.astype(BF16), prefix, preferred_element_type=F32)[0:1]
    total = jnp.dot(count8.astype(BF16), jnp.where(together, 1.0, 0.0).astype(BF16), preferred_element_type=F32)[0:1]
    device = (col_ids((1, lanes)) // local_experts * BASE).astype(F32)
    aligned_row = rank + (aligned_off + device) + 1.0
    exact_row = rank + (exact_off + device) + 1.0
    aligned = jnp.zeros((seq_len, lanes), F32)
    exact = jnp.zeros((seq_len, lanes), F32)
    for j in range(top_k):
        aligned += jnp.where(lane == j, jnp.sum(hits[j] * aligned_row, axis=1, keepdims=True), 0.0)
        exact += jnp.where(lane == j, jnp.sum(hits[j] * exact_row, axis=1, keepdims=True), 0.0)
    table_ref[0] = (jnp.transpose(aligned, (1, 0))[:8]).astype(I32) - 1
    table_ref[0, COUNT_ROW : COUNT_ROW + 1, :lanes] = count8[:1].astype(I32)
    table_ref[0, MOST_ROW : MOST_ROW + 1, :lanes] = jnp.broadcast_to(
        jnp.max(total, axis=1, keepdims=True), (1, lanes)
    ).astype(I32)
    exact_ref[0] = exact[:, :8].astype(I32) - 1


def route(experts, slots, local_experts, group):
    batches, seq_len, top_k = experts.shape
    return pl.pallas_call(
        functools.partial(route_kernel, local_experts, top_k),
        grid=(batches,),
        in_specs=[pl.BlockSpec((1, seq_len, top_k), by_place)] * 2,
        out_specs=[
            pl.BlockSpec((1, 8, seq_len), by_place),
            pl.BlockSpec((1, seq_len, 8), by_place),
        ],
        out_shape=[
            jax.ShapeDtypeStruct((batches, 8, seq_len), I32),
            jax.ShapeDtypeStruct((batches, seq_len, 8), I32),
        ],
        compiler_params=pltpu.CompilerParams(vmem_limit_bytes=VMEM_LIMIT // 2),
        cost_estimate=SMALL,
        name="route",
    )(experts, slots)


def front_kernel(
    group, top_k, head_dim,
    xa_ref, xb_ref, q_ref, k_ref, v_ref, wo_ref, mgain_ref, table_ref,
    ha_ref, hb_ref, ua_ref, ub_ref, tables_ref, xs_ref,
    qkv, wo, xbuf, acc, hbuf, ubuf, codes, urows, xrows, picks,
    q_sem, w_sem, x_sem, h_sem, u_sem, t_sem, load_sem, put_sem, send_sem, recv_sem, tsend_sem, trecv_sem,
):
    seq_len, model_dim = xbuf.shape
    half = seq_len // 2
    pairs = wo.shape[0]
    scale = head_dim**-0.5
    chips = group // 2
    me = lax.axis_index("ep")
    chip, core = me // 2, lax.rem(me, 2)
    mate = chip * 2 + 1 - core
    left = lax.rem(chip + chips - 1, chips) * 2 + core
    right = lax.rem(chip + 1, chips) * 2 + core
    far = lax.rem(chip + 2, chips) * 2 + core

    def weight_copy(p):
        return pltpu.make_async_copy(wo_ref.at[p], wo.at[p], w_sem.at[p])

    def qkv_copies(b):
        rows = pl.ds(b * seq_len, seq_len)
        return [
            pltpu.make_async_copy(src.at[:, rows], qkv.at[b, i], q_sem.at[b, i])
            for i, src in enumerate((q_ref, k_ref, v_ref))
        ]

    load_a = pltpu.make_async_copy(xa_ref, xbuf, x_sem.at[0])
    load_b = pltpu.make_async_copy(xb_ref, xbuf, x_sem.at[1])
    load_a.start()
    for c in qkv_copies(0):
        c.start()

    def start_weights(p, _):
        weight_copy(p).start()
        return 0

    repeat(pairs, start_weights)

    barrier = pltpu.get_barrier_semaphore()
    for d in range(1, group):
        pl.semaphore_signal(barrier, device_id={"ep": lax.rem(me + d, group)}, device_id_type=pl.DeviceIdType.MESH)
    pl.semaphore_wait(barrier, group - 1)

    def table_copy(d, slot):
        return pltpu.make_async_remote_copy(
            src_ref=table_ref, dst_ref=tables_ref.at[slot], send_sem=tsend_sem.at[d], recv_sem=trecv_sem.at[d],
            device_id={"ep": lax.rem(me + d, group)}, device_id_type=pl.DeviceIdType.MESH,
        )

    own_table = pltpu.make_async_copy(table_ref, tables_ref.at[me], t_sem.at[0])
    own_table.start()
    for d in range(1, group):
        table_copy(d, me).start()

    part0, part1, both = pl.ds(0, half), pl.ds(half, half), pl.ds(0, seq_len)

    def u_copy(k, whose, rows, to):
        return pltpu.make_async_remote_copy(
            src_ref=ua_ref.at[whose, rows], dst_ref=ua_ref.at[whose, rows], send_sem=send_sem.at[k],
            recv_sem=recv_sem.at[k], device_id={"ep": to}, device_id_type=pl.DeviceIdType.MESH,
        )

    def mate_of(device):
        return device // 2 * 2 + 1 - lax.rem(device, 2)

    sends = [
        (me, part0, right), (me, part1, right), (me, part1, left), (me, part0, left),
        (left, part0, right), (right, part1, left), (me, both, mate),
        (left, part0, mate), (left, part1, mate), (right, part1, mate), (right, part0, mate),
        (far, part0, mate), (far, part1, mate),
    ]
    received = [
        left, left, right, right, far, far, mate,
        mate_of(left), mate_of(left), mate_of(right), mate_of(right), mate_of(far), mate_of(far),
    ]

    def send(k):
        u_copy(k, *sends[k]).start()

    def arrived(k):
        u_copy(k, received[k], sends[k][1], sends[k][2]).wait_recv()

    def attend_head(q, k, v, first_row):
        scores = lax.dot_general(q, k, (((1,), (1,)), ((), ())), preferred_element_type=F32) * scale
        rows = row_ids(scores.shape) + first_row
        cols = col_ids(scores.shape)
        scores = jnp.where(rows >= cols, scores, MASK_VALUE)
        top = jnp.max(scores, axis=-1, keepdims=True)
        e = jnp.exp(scores - top)
        prob = (e * (1.0 / jnp.sum(e, axis=-1, keepdims=True))).astype(BF16)
        return jnp.dot(prob, v, preferred_element_type=F32).astype(BF16)

    def begin():
        for piece in pieces(seq_len):
            acc[piece] = xbuf[piece].astype(F32)

    def low_half(b, p, n_pairs=1):
        outs = []
        for j in range(n_pairs):
            heads = []
            for i in range(2):
                q, k, v = (qkv.at[b, n, 2 * (p + j) + i] for n in range(3))
                heads.append(attend_head(q[:half], k[:half], v[:half], 0))
            outs.append(jnp.dot(jnp.concatenate(heads, axis=1), wo[p + j], preferred_element_type=F32))
        acc[:half] += functools.reduce(lambda x, y: x + y, outs)

    def high_half(b, p, n_pairs=1):
        outs = []
        for j in range(n_pairs):
            heads = []
            for i in range(2):
                q, k, v = (qkv.at[b, n, 2 * (p + j) + i] for n in range(3))
                heads.append(attend_head(q[half:], k[...], v[...], half))
            outs.append(jnp.dot(jnp.concatenate(heads, axis=1), wo[p + j], preferred_element_type=F32))
        acc[half:] += functools.reduce(lambda x, y: x + y, outs)

    def finish(first, last):
        gain = mgain_ref[...].astype(F32)
        for piece in pieces(last, first):
            h = acc[piece].astype(BF16)
            hbuf[piece] = h
            ubuf[piece] = rms_rows(h.astype(F32), gain)

    load_a.wait()
    begin()
    load_b.start()
    for c in qkv_copies(0):
        c.wait()
    for c in qkv_copies(1):
        c.start()

    def low_a(p, _):
        weight_copy(2 * p).wait()
        weight_copy(2 * p + 1).wait()
        low_half(0, 2 * p, 2)
        return 0

    def high_a(p, _):
        high_half(0, 2 * p, 2)
        return 0

    def put_part(part, i):
        return pltpu.make_async_copy(ubuf.at[part], ua_ref.at[me, part], u_sem.at[i])

    repeat(pairs // 2, low_a)
    finish(0, half)
    put_part(part0, 0).start()
    put_part(part0, 0).wait()
    send(0)
    send(3)
    repeat(pairs // 2, high_a)
    finish(half, seq_len)
    put_part(part1, 2).start()
    put_part(part1, 2).wait()
    send(2)
    send(1)
    send(6)
    put_h = pltpu.make_async_copy(hbuf, ha_ref, h_sem.at[0])
    put_h.start()

    load_b.wait()
    begin()
    for c in qkv_copies(1):
        c.wait()

    def pair_b(p, _):
        low_half(1, p)
        high_half(1, p)

        @pl.when(p == pairs - 1)
        def _():
            arrived(0)
            send(4)
            send(7)
            arrived(2)
            send(5)
            send(9)

        return 0

    repeat(pairs, pair_b)
    put_h.wait()
    finish(0, seq_len)
    put_ub = pltpu.make_async_copy(ubuf, ub_ref, u_sem.at[1])
    put_hb = pltpu.make_async_copy(hbuf, hb_ref, h_sem.at[1])
    put_ub.start()
    put_hb.start()

    own_table.wait()
    for d in range(1, group):
        table_copy(d, lax.rem(me + group - d, group)).wait_recv()
    load_codes = pltpu.make_async_copy(tables_ref.at[:, 0], codes, t_sem.at[1])
    load_codes.start()
    load_codes.wait()
    chunks, chunk = xrows.shape[1:3]

    def load(source, slot):
        return pltpu.make_async_copy(ua_ref.at[source], urows.at[slot], load_sem.at[slot])

    def build(source, slot):
        code = codes[source] - me * BASE

        def chunk_of(i, _):
            row = row_ids((chunk, seq_len)) + i * chunk
            pick = jnp.zeros((chunk, seq_len), F32)
            for j in range(top_k):
                pick = jnp.where(row == code[j : j + 1, :], 1.0, pick)
            picks[slot, pl.ds(pl.multiple_of(i * chunk, chunk), chunk)] = pick.astype(BF16)
            return 0

        repeat(chunks, chunk_of)

    def put_rows(source, i, slot):
        rows = pl.ds(pl.multiple_of(i * chunk, chunk), chunk)
        return pltpu.make_async_copy(xrows.at[slot, i], xs_ref.at[source, rows], put_sem.at[slot, i])

    def select(source, slot, first, last):
        def chunk_of(i, _):
            pick = picks[slot, pl.ds(pl.multiple_of(i * chunk, chunk), chunk)]
            xrows[slot, i] = jnp.dot(pick, urows[slot], preferred_element_type=F32).astype(BF16)
            put_rows(source, i, slot).start()
            return 0

        lax.fori_loop(first, last, chunk_of, 0)

    def put_done(source, slot):
        for i in range(chunks):
            put_rows(source, i, slot).wait()

    def source_at(i):
        return lax.rem(chip + lax.rem(i // 2 * 3, 5), chips) * 2 + lax.rem(core + i, 2)

    def near(i, _):
        slot = lax.rem(i, 2)
        source = source_at(i)

        @pl.when(i == 1)
        def _():
            arrived(6)

        @pl.when(i == 2)
        def _():
            arrived(1)
            send(8)
            arrived(3)
            send(10)

        @pl.when(i == 3)
        def _():
            arrived(7)
            arrived(8)

        @pl.when(i == 5)
        def _():
            arrived(9)
            arrived(10)

        load(source, slot).start()
        build(source, slot)

        @pl.when(i >= 2)
        def _():
            put_done(source_at(i - 2), slot)

        load(source, slot).wait()
        select(source, slot, 0, chunks)
        return 0

    repeat(6, near)
    build(far, 0)
    build(mate_of(far), 1)
    put_done(source_at(4), 0)
    put_done(source_at(5), 1)
    arrived(4)
    send(11)
    arrived(5)
    send(12)
    load(far, 0).start()
    load(far, 0).wait()
    select(far, 0, 0, 1)
    arrived(11)
    arrived(12)
    load(mate_of(far), 1).start()
    select(far, 0, 1, chunks)
    load(mate_of(far), 1).wait()
    select(mate_of(far), 1, 0, chunks)
    put_done(far, 0)
    put_done(mate_of(far), 1)

    for k in range(len(sends)):
        u_copy(k, *sends[k]).wait_send()
    for d in range(1, group):
        table_copy(d, me).wait_send()
    put_ub.wait()
    put_hb.wait()


def front(xa, xb, w_query, w_key, w_value, w_out, attn_gain, moe_gain, table, group, top_k, full_rows):
    seq_len, model_dim = xa.shape
    heads, head_dim = w_query.shape[1:]
    pairs = heads // 2
    wide = 2 * head_dim
    x = jnp.concatenate([xa, xb], axis=0)
    normed = rms_rows(x.astype(F32), attn_gain.astype(F32))
    q, k, v = (
        jnp.einsum("td,dhe->hte", normed, w, preferred_element_type=F32).astype(BF16) for w in (w_query, w_key, w_value)
    )
    wo = w_out.reshape(pairs, wide, model_dim)
    rows = jax.ShapeDtypeStruct((seq_len, model_dim), BF16)
    anywhere = pl.BlockSpec(memory_space=pl.ANY)
    vmem = pl.BlockSpec(memory_space=pltpu.VMEM)
    dma = pltpu.SemaphoreType.DMA
    pair = dma((2,))
    chunk = 256
    return pl.pallas_call(
        functools.partial(front_kernel, group, top_k, head_dim),
        in_specs=[anywhere] * 6 + [vmem] * 2,
        out_specs=[anywhere] * 6,
        out_shape=[
            rows,
            rows,
            jax.ShapeDtypeStruct((group, seq_len, model_dim), BF16),
            rows,
            jax.ShapeDtypeStruct((group,) + table.shape, I32),
            jax.ShapeDtypeStruct((group, full_rows, model_dim), BF16),
        ],
        scratch_shapes=[
            pltpu.VMEM((2, 3, heads, seq_len, head_dim), BF16),
            pltpu.VMEM((pairs, wide, model_dim), BF16),
            pltpu.VMEM((seq_len, model_dim), BF16),
            pltpu.VMEM((seq_len, model_dim), F32),
            pltpu.VMEM((seq_len, model_dim), BF16),
            pltpu.VMEM((seq_len, model_dim), BF16),
            pltpu.VMEM((group,) + table.shape[1:], I32),
            pltpu.VMEM((2, seq_len, model_dim), BF16),
            pltpu.VMEM((2, full_rows // chunk, chunk, model_dim), BF16),
            pltpu.VMEM((2, full_rows, seq_len), BF16),
            dma((2, 3)),
            dma((pairs,)),
            pair,
            pair,
            dma((3,)),
            pair,
            pair,
            dma((2, full_rows // chunk)),
            dma((13,)),
            dma((13,)),
            dma((group,)),
            dma((group,)),
        ],
        compiler_params=pltpu.CompilerParams(vmem_limit_bytes=VMEM_LIMIT, collective_id=0, has_side_effects=True),
        cost_estimate=pl.CostEstimate(
            flops=2 * (8 * seq_len * model_dim * model_dim + 4 * seq_len * seq_len * model_dim),
            bytes_accessed=2 * 4 * model_dim * model_dim,
            transcendentals=2 * heads * seq_len * seq_len,
        ),
        name="front",
    )(xa, xb, q, k, v, wo, moe_gain.reshape(1, -1), table)


def select_kernel(top_k, me_ref, code_ref, u_ref, out_ref):
    aligned_rows, seq_len = out_ref.shape[1], u_ref.shape[1]
    code = code_ref[0] - me_ref[0] * BASE
    chunk = aligned_rows if aligned_rows <= 512 else 256
    for first in range(0, aligned_rows, chunk):
        row = row_ids((chunk, seq_len)) + first
        pick = jnp.zeros((chunk, seq_len), F32)
        for j in range(top_k):
            pick = jnp.where(row == code[j : j + 1, :], 1.0, pick)
        out_ref[0, first : first + chunk] = jnp.dot(pick.astype(BF16), u_ref[0], preferred_element_type=F32).astype(BF16)


def select_rows(me, codes, u_all, aligned_rows, top_k):
    group, seq_len, model_dim = u_all.shape
    return pl.pallas_call(
        functools.partial(select_kernel, top_k),
        grid_spec=pltpu.PrefetchScalarGridSpec(
            num_scalar_prefetch=1,
            grid=(group,),
            in_specs=[
                pl.BlockSpec((1, 8, seq_len), by_place),
                pl.BlockSpec((1, seq_len, model_dim), by_place),
            ],
            out_specs=pl.BlockSpec((1, aligned_rows, model_dim), by_place),
        ),
        out_shape=jax.ShapeDtypeStruct((group, aligned_rows, model_dim), BF16),
        compiler_params=pltpu.CompilerParams(vmem_limit_bytes=VMEM_LIMIT),
        cost_estimate=pl.CostEstimate(
            flops=2 * group * aligned_rows * seq_len * model_dim,
            bytes_accessed=2 * group * (aligned_rows + seq_len) * model_dim,
            transcendentals=NONE,
        ),
        name="select",
    )(me, codes, u_all)


def expert_kernel(
    segment_sizes, me_ref, count_ref, x_in, gate_ref, up_ref, down_ref, x_out,
    buf, blocks_ref, offset_ref, total_ref, in_sem, out_sem,
):
    step = pl.program_id(0)
    steps = pl.num_programs(0)
    places = x_in.shape[0]

    def each_segment(expert, slot, fn):
        def per_place(place, filled):
            n = blocks_ref[place, expert]
            first = offset_ref[place, expert]
            for size in segment_sizes:

                @pl.when(n // size % 2 == 1)
                def _():
                    done = n // (2 * size) * (2 * size)
                    rows = pl.ds(pl.multiple_of(first + done * BLOCK, BLOCK), size * BLOCK)
                    held = pl.ds(pl.multiple_of((filled + done) * BLOCK, BLOCK), size * BLOCK)
                    fn(place, rows, buf.at[slot, held], slot)

            return filled + n

        lax.fori_loop(0, places, per_place, jnp.int32(0))

    def fetch(place, rows, held, slot):
        pltpu.make_async_copy(x_in.at[place, rows], held, in_sem.at[slot]).start()

    def put(place, rows, held, slot):
        pltpu.make_async_copy(held, x_out.at[place, rows], out_sem.at[slot]).start()

    def fetched(n, slot):
        rows = pl.ds(0, n * BLOCK)
        pltpu.make_async_copy(x_in.at[0, rows], buf.at[slot, rows], in_sem.at[slot]).wait()

    def gone(n, slot):
        rows = pl.ds(0, n * BLOCK)
        pltpu.make_async_copy(buf.at[slot, rows], x_out.at[0, rows], out_sem.at[slot]).wait()

    def over(expert, fn):
        each_segment(expert, lax.rem(expert, 3), fn)

    def wait_all(expert, fn):
        slot = lax.rem(expert, 3)
        n = total_ref[expert]

        def most(i, _):
            fn(16, slot)
            return 0

        repeat(n // 16, most)
        for size in (8, 4, 2, 1):

            @pl.when(n // size % 2 == 1)
            def _():
                fn(size, slot)

        return n

    @pl.when(step == 0)
    def _():
        def plan(place, _):
            def one(e, filled):
                n = (count_ref[place, me_ref[0] * steps + e] + (BLOCK - 1)) // BLOCK
                blocks_ref[place, e] = n
                offset_ref[place, e] = filled * BLOCK
                total_ref[e] = jnp.where(place == 0, 0, total_ref[e]) + n
                return filled + n

            lax.fori_loop(0, steps, one, jnp.int32(0))
            return 0

        repeat(places, plan)
        over(step, fetch)

    @pl.when(step >= 2)
    def _():
        wait_all(step - 2, gone)

    @pl.when(step + 1 < steps)
    def _():
        over(step + 1, fetch)

    filled = wait_all(step, fetched)
    slot = lax.rem(step, 3)

    def tile(i, _):
        rows = pl.ds(pl.multiple_of(i * TILE, TILE), TILE)
        x = buf[slot, rows]
        gate = jnp.dot(x, gate_ref[0], preferred_element_type=F32)
        up = jnp.dot(x, up_ref[0], preferred_element_type=F32)
        hidden = (gate * jax.nn.sigmoid(gate) * up).astype(BF16)
        buf[slot, rows] = jnp.dot(hidden, down_ref[0], preferred_element_type=F32).astype(BF16)
        return 0

    repeat((filled * BLOCK + TILE - 1) // TILE, tile)
    over(step, put)

    @pl.when(step + 1 == steps)
    def _():
        wait_all(step - 1, gone)
        wait_all(step, gone)


def expert_ffn(me, counts, x, w_gate, w_up, w_down, capacity):
    places, aligned_rows, model_dim = x.shape
    experts, _, hidden_dim = w_gate.shape
    held = -(-places * capacity // TILE) * TILE
    most = -(-capacity // BLOCK)
    segment_sizes = [1 << i for i in reversed(range(most.bit_length()))]
    weight_in = pl.BlockSpec((1, model_dim, hidden_dim), by_place)
    return pl.pallas_call(
        functools.partial(expert_kernel, segment_sizes),
        grid_spec=pltpu.PrefetchScalarGridSpec(
            num_scalar_prefetch=2,
            grid=(experts,),
            in_specs=[
                pl.BlockSpec(memory_space=pl.ANY),
                weight_in,
                weight_in,
                pl.BlockSpec((1, hidden_dim, model_dim), by_place),
            ],
            out_specs=pl.BlockSpec(memory_space=pl.ANY),
            scratch_shapes=[
                pltpu.VMEM((3, held, model_dim), BF16),
                pltpu.SMEM((places, experts), I32),
                pltpu.SMEM((places, experts), I32),
                pltpu.SMEM((experts,), I32),
                pltpu.SemaphoreType.DMA((3,)),
                pltpu.SemaphoreType.DMA((3,)),
            ],
        ),
        out_shape=jax.ShapeDtypeStruct(x.shape, BF16),
        input_output_aliases={2: 0},
        compiler_params=pltpu.CompilerParams(vmem_limit_bytes=VMEM_LIMIT),
        cost_estimate=pl.CostEstimate(
            flops=6 * 3072 * model_dim * hidden_dim,
            bytes_accessed=6 * experts * model_dim * hidden_dim,
            transcendentals=NONE,
        ),
        name="experts",
    )(me, counts, x, w_gate, w_up, w_down)


def pack_kernel(local_experts, me_ref, count_ref, x_ref, out_ref):
    rows_out, aligned_rows = out_ref.shape[1], x_ref.shape[1]
    place = pl.program_id(0)
    chunk = rows_out if rows_out <= 512 else 256
    for first in range(0, rows_out, chunk):
        row = row_ids((chunk, 1)) + first
        source = jnp.full((chunk, 1), -1, I32)
        off, aligned_off = jnp.int32(0), jnp.int32(0)
        for e in range(local_experts):
            n = count_ref[place, me_ref[0] * local_experts + e]
            inside = (row >= off) & (row < off + n)
            source = jnp.where(inside, row + (aligned_off - off), source)
            off = off + n
            aligned_off = aligned_off + (n + (BLOCK - 1)) // BLOCK * BLOCK
        col = col_ids((chunk, aligned_rows))
        pick = jnp.where(col == source, 1.0, 0.0).astype(BF16)
        out_ref[0, first : first + chunk] = jnp.dot(pick, x_ref[0], preferred_element_type=F32).astype(BF16)


def pack_rows(me, counts, x, local_experts, aligned_rows, rows_out):
    places, _, model_dim = x.shape
    return pl.pallas_call(
        functools.partial(pack_kernel, local_experts),
        grid_spec=pltpu.PrefetchScalarGridSpec(
            num_scalar_prefetch=2,
            grid=(places,),
            in_specs=[pl.BlockSpec((1, aligned_rows, model_dim), by_place)],
            out_specs=pl.BlockSpec((1, rows_out, model_dim), by_place),
        ),
        out_shape=jax.ShapeDtypeStruct((places, rows_out, model_dim), BF16),
        compiler_params=pltpu.CompilerParams(vmem_limit_bytes=VMEM_LIMIT),
        cost_estimate=pl.CostEstimate(
            flops=2 * places * aligned_rows * rows_out * model_dim,
            bytes_accessed=2 * places * (aligned_rows + rows_out) * model_dim,
            transcendentals=NONE,
        ),
        name="pack",
    )(me, counts, x)


def combine_kernel(top_k, code_ref, gates_ref, recv_ref, h_ref, out_ref, acc_ref):
    step = pl.program_id(0)
    rows = recv_ref.shape[0]

    @pl.when(step == 0)
    def _():
        acc_ref[...] = h_ref[...].astype(F32)

    code = code_ref[...]
    gates = gates_ref[...]
    col = col_ids((code.shape[0], rows)) + step * rows
    mix = jnp.zeros(col.shape, F32)
    for j in range(top_k):
        mix = jnp.where(col == code[:, j : j + 1], gates[:, j : j + 1], mix)
    acc_ref[...] += jnp.dot(mix.astype(BF16), recv_ref[...], preferred_element_type=F32)

    @pl.when(step == pl.num_programs(0) - 1)
    def _():
        out_ref[...] = acc_ref[...].astype(BF16)


def combine(residual, recv, code, gates):
    seq_len, model_dim = residual.shape
    group, rows, _ = recv.shape
    top_k = gates.shape[1]
    column = jnp.where(code >= 0, code // BASE * rows + code % BASE, -1)
    gates_f = jnp.pad(gates.astype(F32), ((0, 0), (0, 8 - top_k)))
    rows_step = 256
    whole = lambda r, c: pl.BlockSpec((r, c), at_origin)
    return pl.pallas_call(
        functools.partial(combine_kernel, top_k),
        grid=(group * rows // rows_step,),
        in_specs=[
            whole(seq_len, 8),
            whole(seq_len, 8),
            pl.BlockSpec((rows_step, model_dim), lambda i: (i, 0)),
            whole(seq_len, model_dim),
        ],
        out_specs=whole(seq_len, model_dim),
        out_shape=jax.ShapeDtypeStruct((seq_len, model_dim), BF16),
        scratch_shapes=[pltpu.VMEM((seq_len, model_dim), F32)],
        compiler_params=pltpu.CompilerParams(vmem_limit_bytes=VMEM_LIMIT),
        cost_estimate=pl.CostEstimate(
            flops=2 * seq_len * group * rows * model_dim,
            bytes_accessed=2 * (group * rows + 2 * seq_len) * model_dim,
            transcendentals=NONE,
        ),
        name="combine",
    )(column, gates_f, recv.reshape(group * rows, model_dim), residual)


def back_kernel(
    group, top_k, packed_ref, got_ref, codes_ref, gates_ref, ha_ref, hb_ref, outa_ref, outb_ref,
    recv, held, acc, own_sem, held_sem, send_sem, recv_sem,
):
    seq_len, model_dim = ha_ref.shape
    rows = recv.shape[1]
    chips = group // 2
    me = lax.axis_index("ep")
    chip, core = me // 2, lax.rem(me, 2)

    def device_at(place):
        pair = place // 2
        away = pair + pair // 2 - 2 * (pair // 3)
        return lax.rem(chip + away, chips) * 2 + lax.rem(core + place, 2)

    def copy(place):
        seen = (0, 1, 4, 5, 2, 3, 6, 7)[place]
        to = device_at(place)
        return pltpu.make_async_remote_copy(
            src_ref=packed_ref.at[to], dst_ref=recv.at[me], send_sem=send_sem.at[place], recv_sem=recv_sem.at[seen],
            device_id={"ep": to}, device_id_type=pl.DeviceIdType.MESH,
        )

    def hold(source, slot):
        return pltpu.make_async_copy(got_ref.at[source], held.at[slot], held_sem.at[slot])

    barrier = pltpu.get_barrier_semaphore()
    for d in range(1, group):
        pl.semaphore_signal(barrier, device_id={"ep": lax.rem(me + d, group)}, device_id_type=pl.DeviceIdType.MESH)
    hold(0, 0).start()
    own = pltpu.make_async_copy(packed_ref.at[me], recv.at[me], own_sem)
    own.start()
    pl.semaphore_wait(barrier, group - 1)
    for place in (1, 2, 4, 3, 5, 6, 7):
        copy(place).start()

    def mix_of(batch, source):
        code = codes_ref[batch] - source * BASE
        gates = gates_ref[batch]
        col = col_ids((seq_len, rows))
        mix = jnp.zeros((seq_len, rows), F32)
        for j in range(top_k):
            mix = jnp.where(col == code[:, j : j + 1], gates[:, j : j + 1], mix)
        return mix.astype(BF16)

    def begin(h_ref):
        for piece in pieces(seq_len):
            acc[piece] = h_ref[piece].astype(F32)

    def finish(out_ref):
        for piece in pieces(seq_len):
            out_ref[piece] = acc[piece].astype(BF16)

    begin(ha_ref)

    def add_a(source, _):
        slot = lax.rem(source, 2)

        @pl.when(source + 1 < group)
        def _():
            hold(source + 1, 1 - slot).start()

        mix = mix_of(0, source)
        hold(source, slot).wait()
        acc[...] += jnp.dot(mix, held[slot], preferred_element_type=F32)
        return 0

    repeat(group, add_a)
    finish(outa_ref)
    begin(hb_ref)

    def add_b(place, _):
        source = device_at(place)
        mix = mix_of(1, source)

        @pl.when(place == 0)
        def _():
            own.wait()

        @pl.when(place > 0)
        def _():
            pltpu.make_async_remote_copy(
                src_ref=packed_ref.at[source], dst_ref=recv.at[source], send_sem=send_sem.at[place],
                recv_sem=recv_sem.at[place], device_id={"ep": source}, device_id_type=pl.DeviceIdType.MESH,
            ).wait_recv()

        acc[...] += jnp.dot(mix, recv[source], preferred_element_type=F32)
        return 0

    repeat(group, add_b)
    finish(outb_ref)
    for place in range(1, group):
        copy(place).wait_send()


def return_and_combine(packed_b, back_a, h_a, h_b, codes, gates, group):
    seq_len, model_dim = h_a.shape
    rows = packed_b.shape[1]
    top_k = gates.shape[2]
    gates_f = jnp.pad(gates.astype(F32), ((0, 0), (0, 0), (0, 8 - top_k)))
    vmem = pl.BlockSpec(memory_space=pltpu.VMEM)
    anywhere = pl.BlockSpec(memory_space=pl.ANY)
    dma = pltpu.SemaphoreType.DMA
    pair = dma((2,))
    return pl.pallas_call(
        functools.partial(back_kernel, group, top_k),
        in_specs=[anywhere, anywhere, vmem, vmem, vmem, vmem],
        out_specs=[vmem, vmem],
        out_shape=[jax.ShapeDtypeStruct((seq_len, model_dim), BF16)] * 2,
        scratch_shapes=[
            pltpu.VMEM((group, rows, model_dim), BF16),
            pltpu.VMEM((2, rows, model_dim), BF16),
            pltpu.VMEM((seq_len, model_dim), F32),
            dma,
            pair,
            dma((group,)),
            dma((group,)),
        ],
        compiler_params=pltpu.CompilerParams(vmem_limit_bytes=VMEM_LIMIT, collective_id=1, has_side_effects=True),
        cost_estimate=pl.CostEstimate(
            flops=4 * seq_len * group * rows * model_dim,
            bytes_accessed=2 * (4 * group * rows + 4 * seq_len) * model_dim,
            transcendentals=NONE,
        ),
        name="back",
    )(packed_b, back_a, codes, gates_f, h_a, h_b)


def emit_kernel(a_ref, b_ref, outa_ref, outb_ref):
    outa_ref[...] = a_ref[...]
    outb_ref[...] = b_ref[...]


def emit(a, b):
    seq_len, model_dim = a.shape
    block = pl.BlockSpec((seq_len // 4, model_dim), lambda i: (i, 0))
    return pl.pallas_call(
        emit_kernel,
        grid=(4,),
        in_specs=[block, block],
        out_specs=[block, block],
        out_shape=[jax.ShapeDtypeStruct(a.shape, BF16)] * 2,
        compiler_params=pltpu.CompilerParams(vmem_limit_bytes=VMEM_LIMIT // 2),
        cost_estimate=SMALL,
        name="emit",
    )(a, b)


def capacity_of(seq_len, top_k, experts_total):
    return 8 * max(1, (seq_len * top_k) // (4 * experts_total))


def solution(mesh):
    group = mesh.shape["ep"]
    row_spec = P(("dp", "ep"), None)
    full_spec = P(None, None, None)
    gain_spec = P(None)
    expert_spec = P("ep", None, None)
    in_specs = (row_spec,) * 8 + (gain_spec, full_spec, full_spec, full_spec, full_spec, gain_spec) + (expert_spec,) * 3

    def device_fn(
        tokens_a, experts_a, slots_a, gates_a, tokens_b, experts_b, slots_b, gates_b,
        attn_gain, w_query, w_key, w_value, w_out, moe_gain, w_gate, w_up, w_down,
    ):
        seq_len, model_dim = tokens_a.shape
        local_experts = w_gate.shape[0]
        capacity = capacity_of(seq_len, experts_a.shape[1], local_experts * group)
        full_rows = local_experts * capacity
        me = lax.axis_index("ep").astype(I32)

        top_k = experts_a.shape[1]
        me1 = me.reshape(1)
        table, exact = route(jnp.stack([experts_a, experts_b]), jnp.stack([slots_a, slots_b]), local_experts, group)
        h_a, h_b, u_all_a, u_b, tables, x_a = front(
            tokens_a, tokens_b, w_query, w_key, w_value, w_out, attn_gain, moe_gain, table, group, top_k, full_rows
        )
        counts = tables[:, :, COUNT_ROW, : local_experts * group].transpose(1, 0, 2)
        codes = tables.transpose(1, 0, 2, 3)
        largest = jnp.max(tables[:, :, MOST_ROW, 0])
        packed_rows = 352

        def packed_outputs(x, counts_b, aligned_rows, rows_out):
            o = expert_ffn(me1, counts_b, x, w_gate, w_up, w_down, capacity)
            return pack_rows(me1, counts_b, o, local_experts, aligned_rows, rows_out)

        def usual(operands):
            x_a, u_all_a, u_b, h_a, h_b, codes, counts, exact = operands
            aligned_rows = min(full_rows, -(-(packed_rows + local_experts * (BLOCK - 1)) // 160) * 160)
            u_all_b = lax.all_gather(u_b, "ep", axis=0, tiled=False)
            packed_a = packed_outputs(x_a, counts[0], aligned_rows, packed_rows)
            back_a = lax.all_to_all(packed_a, "ep", 0, 0, tiled=True)
            x_b = select_rows(me1, codes[1], u_all_b, aligned_rows, top_k)
            packed_b = packed_outputs(x_b, counts[1], aligned_rows, packed_rows)
            gates = jnp.stack([gates_a, gates_b])
            return tuple(emit(*return_and_combine(packed_b, back_a, h_a, h_b, exact, gates, group)))

        def fullest(operands):
            x_a, u_all_a, u_b, h_a, h_b, codes, counts, exact = operands
            u_all_b = lax.all_gather(u_b, "ep", axis=0, tiled=False)

            def one(batch):
                u_all, h, codes_b, counts_b, exact_b, gates_b = batch
                x = select_rows(me1, codes_b, u_all, full_rows, top_k)
                back = lax.all_to_all(packed_outputs(x, counts_b, full_rows, full_rows), "ep", 0, 0, tiled=True)
                return combine(h, back, exact_b, gates_b)

            both = lax.map(
                one,
                (jnp.stack([u_all_a, u_all_b]), jnp.stack([h_a, h_b]), codes, counts, exact, jnp.stack([gates_a, gates_b])),
            )
            return both[0], both[1]

        operands = (x_a, u_all_a, u_b, h_a, h_b, codes, counts, exact)
        return lax.cond(largest <= packed_rows, usual, fullest, operands)

    return jax.shard_map(device_fn, mesh=mesh, in_specs=in_specs, out_specs=(row_spec, row_spec), check_vma=False)
```

time: 573 us -> 539 us (0.941)
  waiting for transfers between devices: 120 us -> 12.6 us
  Pallas kernels: 365 us -> 449 us
  loops' own time: 7.81 us -> 0.75 us
    all_to_all x2 -> x1, waiting for transfers between devices: 119 us -> 11.9 us  [usual(): back_a = lax.all_to_all(packed_a, 'ep', 0, 0, tiled=True)]
    pallas_call x4, Pallas kernels: 202 us -> 297 us  [the longest x2 162 us: expert_ffn(): pl.pallas_call(functools.partial(expert_kernel, segment_sizes), grid_spec...]
    pallas_call x1, Pallas kernels: 109 us -> 97.3 us  [front(): pl.pallas_call(functools.partial(front_kernel, group, top_k, head_dim), i...]
    another operation x1, loops' own time: 7.81 us -> 0.75 us  [device_fn(): return lax.cond(largest <= packed_rows, usual, fullest, operands)]
  transfers between devices with their start and end apart: 3 -> 2, of which waited for: 2 -> 1; matrix products, arithmetic and copies ran while one was open for 1% -> 0% of each run, Pallas kernels for 41% -> 40%
where the time goes in v2:
time: 539 us; the launch traced here: 531 us
  Pallas kernels  449 us (83%)
  matrix products  36 us (7%)
  between operations  15.1 us (3%)
  waiting for transfers between devices  12.6 us (2%)
  local copies, waits for them, and re-layouts  6.58 us (1%)
  starting transfers between devices  5.76 us (1%)
    pallas_call x2, Pallas kernels, expert_ffn(): pl.pallas_call(functools.partial(expert_kernel, segment_sizes), grid_spec...  162 us
    pallas_call x1, Pallas kernels, return_and_combine(): pl.pallas_call(functools.partial(back_kernel, group, top_k), in_specs=[an...  133 us
    pallas_call x1, Pallas kernels, front(): pl.pallas_call(functools.partial(front_kernel, group, top_k, head_dim), i...  97.3 us
    dot_general x3, matrix products, front(): jnp.einsum('td,dhe->hte', normed, w, preferred_element_type=F32)  36 us
    pallas_call x2, Pallas kernels, pack_rows(): pl.pallas_call(functools.partial(pack_kernel, local_experts), grid_spec=p...  32 us
    pallas_call x1, Pallas kernels, select_rows(): pl.pallas_call(functools.partial(select_kernel, top_k), grid_spec=pltpu.P...  17.8 us
    all_to_all x1, waiting for transfers between devices, usual(): back_a = lax.all_to_all(packed_a, 'ep', 0, 0, tiled=True)  11.9 us
  transfers between devices with their start and end apart: 2, of which 1 were waited for; matrix products, arithmetic and copies ran while one was open for 0% of the time, Pallas kernels for 40%

profile of v2, /device:TPU:112, one launch (start us, length us, event | category | flops | bytes accessed | tf_op | source)
XLA Modules:
  0.0 530.7 jit_solution(9977948871544320137)
XLA Ops:
  7.2 0.0 slice-start
  7.2 2.8 fusion.12
  10.0 0.7 convert_element_type.42
  10.7 14.1 %convert_bitcast_fusion.v_ref = bf16[16,1024,128]{2,1,0:T(8,128)(2,1)} fusion(bf16[2048,16,128]{2,1,0:T(8,128)(2,1)} %param.32, f32[2048]{0:T(1024)S(1)} %convert_element_type.42, f32[1024]{0:T(1024)S(1)} %add_rsqrt_fusion, bf16[512,2048]{1,0:T(8,128)(2,1)} %xb_ref.1, bf16[512,2048]{1,0:T(8,128)(2,1)} %xa_ref.1), kind=kOutput, calls=%fused_computation.49 | convolution fusion | flops 8606711808 | bytes 16789504 | tf_op jit(solution)/shard_map/td,dhe->hte/dot_general | solution.py:419
  24.9 0.0 slice-done
  24.9 0.0 copy-done.3
  24.9 0.0 copy-done.4
  24.9 0.0 slice-done.1
  24.9 0.0 slice-start.3
  24.9 10.8 %convert_bitcast_fusion.1.k_ref = bf16[16,1024,128]{2,1,0:T(8,128)(2,1)} fusion(bf16[2048,16,128]{2,1,0:T(8,128)(2,1)S(1)} %bitcast.115, f32[2048]{0:T(1024)S(1)} %convert_element_type.42, f32[1024]{0:T(1024)S(1)} %add_rsqrt_fusion, bf16[512,2048]{1,0:T(8,128)(2,1)S(1)} %copy-done.4, bf16[512,2048]{1,0:T(8,128)(2,1)S(1)} %copy-done.3), kind=kOutput, calls=%fused_computation.50 | convolution fusion | flops 8606711808 | bytes 16789504 | tf_op jit(solution)/shard_map/td,dhe->hte/dot_general | solution.py:419
  35.7 0.0 slice-done.2
  35.7 0.0 slice-done.3
  35.7 0.0 copy-start.8
  35.8 0.0 copy-start.9
  35.8 0.0 copy-start.10
  35.8 0.0 copy-start.11
  35.8 11.1 %convert_bitcast_fusion.2.q_ref = bf16[16,1024,128]{2,1,0:T(8,128)(2,1)} fusion(bf16[2048,16,128]{2,1,0:T(8,128)(2,1)S(1)} %bitcast.117, f32[2048]{0:T(1024)S(1)} %convert_element_type.42, f32[1024]{0:T(1024)S(1)} %add_rsqrt_fusion, bf16[512,2048]{1,0:T(8,128)(2,1)S(1)} %copy-done.4, bf16[512,2048]{1,0:T(8,128)(2,1)S(1)} %copy-done.3), kind=kOutput, calls=%fused_computation.51 | convolution fusion | flops 8606711808 | bytes 16789504 | tf_op jit(solution)/shard_map/td,dhe->hte/dot_general | solution.py:419
  46.9 0.0 copy-done.7
  47.0 0.2 copy.75.experts_ref
  47.3 0.2 copy.76.slots_ref
  47.5 4.3 route.1
  51.8 0.0 copy-start.2
  51.9 0.6 copy-done.2
  52.5 0.6 reshape.28.mgain_ref
  53.1 97.3 %front.1 = (bf16[512,2048]{1,0:T(8,128)(2,1)}, bf16[512,2048]{1,0:T(8,128)(2,1)}, bf16[8,512,2048]{2,1,0:T(8,128)(2,1)}, bf16[512,2048]{1,0:T(8,128)(2,1)}, s32[...) custom-call(bf16[512,2048]{1,0:T(8,128)(2,1)} %xa_ref.1, bf16[512,2048]{1,0:T(8,128)(2,1)} %xb_ref.1, ...), custom_call_target="tpu_custom_call" | custom-call | flops 38654705664 | bytes 33554432 | tf_op jit(solution)/shard_map/front/pallas_call | solution.py:428
  150.4 0.7 slice_reduce_fusion
  151.7 0.0 copy-done.5
  151.7 0.0 copy-done.6
  151.8 371.9 %conditional.1 = ((bf16[512,2048]{1,0:T(8,128)(2,1)}, bf16[512,2048]{1,0:T(8,128)(2,1)})) conditional(s32[]{:T(128)} %convert_element_type.50, (bf16[8,512,2048]{2,1,0:T(8,128)(2,1)}, bf16[512,2048]{1,0:T(8,128)(2,1)}, bf16[512,2048]{1,0:T(8,128)(2,1)}, bf16[512,2048]{1,0:T(8,128)(2,1)}, bf16[512,6]{0,1:T(8,128)(2,1)S(1)}, ...), branch_computations={%region_2.5_spmd, %region_5.6_spmd} | conditional | flops 137238683648 | bytes 527733440 | solution.py:958
  152.0 0.1 all-gather.7.cloned.1.call-start
  152.1 0.7 all-gather.7.cloned.1.call-update
  152.8 0.6 slice_bitcast_fusion.3
  153.4 80.7 %experts.4.x_ref = bf16[8,768,2048]{2,1,0:T(8,128)(2,1)} custom-call(s32[1]{0:T(128)} %get-tuple-element.214.me_ref, s32[8,64]{1,0:T(8,128)} %get-tuple-element.417.count_ref, bf16[8,768,2048]{2,1,0:T(8,128)(2,1)} %get-tuple-element.221.x_in, bf16[8,2048,1408]{2,1,0:T(8,128)(2,1)} %get-tuple-element.218.gate_ref, ...), custom_call_target="tpu_custom_call", output_to_operand_aliasing={{}: (2, {})} | custom-call | flops 53150220288 | bytes 138412032 | tf_op jit(solution)/shard_map/cond/branch_1_fun/experts/pallas_call | solution.py:621
  234.1 16.0 %pack.7 = bf16[8,352,2048]{2,1,0:T(8,128)(2,1)} custom-call(s32[1]{0:T(128)} %get-tuple-element.214.me_ref, s32[8,64]{1,0:T(8,128)} %get-tuple-element.417.count_ref, bf16[8,768,2048]{2,1,0:T(8,128)(2,1)} %experts.4.x_ref), custom_call_target="tpu_custom_call" | custom-call | flops 5536481280 | bytes 27262976 | tf_op jit(solution)/shard_map/cond/branch_1_fun/pack/pallas_call | solution.py:675
  250.1 5.7 %all-to-all-start = ((bf16[8,352,2048]{2,1,0:T(8,128)(2,1)}), bf16[8,352,2048]{2,1,0:T(8,128)(2,1)}, u32[]{:S(2)}, u32[]{:S(2)}) async-start(bf16[8,352,2048]{2,1,0:T(8,128)(2,1)} %pack.7), calls=%async_computation | async-start | bytes 23068672 | tf_op jit(solution)/shard_map/cond/branch_1_fun/all_to_all | solution.py:935
  255.8 0.2 copy.70
  256.0 0.2 copy.71
  256.1 0.9 fusion.11.gates_ref
  257.0 0.7 slice_bitcast_fusion.2.code_ref
  257.7 17.8 %select.30.x_in = bf16[8,480,2048]{2,1,0:T(8,128)(2,1)} custom-call(s32[1]{0:T(128)} %get-tuple-element.214.me_ref, s32[8,8,512]{2,1,0:T(8,128)} %slice_bitcast_fusion.2.code_ref, bf16[8,512,2048]{2,1,0:T(8,128)(2,1)} %bitcast.98), custom_call_target="tpu_custom_call" | custom-call | flops 8053063680 | bytes 32505856 | tf_op jit(solution)/shard_map/cond/branch_1_fun/select/pallas_call | solution.py:488
  275.5 80.9 %experts.3.x_ref = bf16[8,480,2048]{2,1,0:T(8,128)(2,1)} custom-call(s32[1]{0:T(128)} %get-tuple-element.214.me_ref, s32[8,64]{1,0:T(8,128)} %get-tuple-element.418.count_ref, bf16[8,480,2048]{2,1,0:T(8,128)(2,1)} %select.30.x_in, bf16[8,2048,1408]{2,1,0:T(8,128)(2,1)} %get-tuple-element.218.gate_ref, ...), custom_call_target="tpu_custom_call", output_to_operand_aliasing={{}: (2, {})} | custom-call | flops 53150220288 | bytes 138412032 | tf_op jit(solution)/shard_map/cond/branch_1_fun/experts/pallas_call | solution.py:621
  356.4 16.0 %pack.6.packed_ref = bf16[8,352,2048]{2,1,0:T(8,128)(2,1)} custom-call(s32[1]{0:T(128)} %get-tuple-element.214.me_ref, s32[8,64]{1,0:T(8,128)} %get-tuple-element.418.count_ref, bf16[8,480,2048]{2,1,0:T(8,128)(2,1)} %experts.3.x_ref), custom_call_target="tpu_custom_call" | custom-call | flops 5536481280 | bytes 27262976 | tf_op jit(solution)/shard_map/cond/branch_1_fun/pack/pallas_call | solution.py:675
  372.3 11.9 %all-to-all-done.got_ref = bf16[8,352,2048]{2,1,0:T(8,128)(2,1)} async-done(((bf16[8,352,2048]{2,1,0:T(8,128)(2,1)}), bf16[8,352,2048]{2,1,0:T(8,128)(2,1)}, u32[]{:S(2)}, u32[]{:S(2)}) %all-to-all-start) | async-done | bytes 11534368 | tf_op jit(solution)/shard_map/cond/branch_1_fun/all_to_all | solution.py:935
  384.2 133.4 %back.1 = (bf16[512,2048]{1,0:T(8,128)(2,1)}, bf16[512,2048]{1,0:T(8,128)(2,1)}) custom-call(bf16[8,352,2048]{2,1,0:T(8,128)(2,1)} %pack.6.packed_ref, bf16[8,352,2048]{2,1,0:T(8,128)(2,1)} %all-to-all-done.got_ref, s32[2,512,8]{2,1,0:T(8,128)S(1)} %get-tuple-element.222.codes_ref, f32[2,512,8]{2,1,0:T(8,128)} %fusion.11.gates_ref, ...), custom_call_target="tpu_custom_call" | custom-call | flops 11811160064 | bytes 54525952 | tf_op jit(solution)/shard_map/cond/branch_1_fun/back/pallas_call | solution.py:849
  517.7 0.0 copy-start
  517.7 1.6 copy-done
  519.3 1.6 copy-done.1
  520.8 2.4 emit.1
  (24 shorter events, 0.1 us)
Async XLA Ops:
  7.2 17.7 %slice-start = ((s8[8388608]{0:T(1024)(128)(4,1)}), s8[4194304]{0:T(1024)(128)(4,1)S(1)}, s32[]{:S(2)}) async-start(s8[8388608]{0:T(1024)(128)(4,1)} %bitcast.114), calls=%async_computation.4 | async-start | bytes 8388608
  10.7 14.1 %copy-start.3 = (bf16[512,2048]{1,0:T(8,128)(2,1)S(1)}, bf16[512,2048]{1,0:T(8,128)(2,1)}, u32[]{:S(2)}) copy-start(bf16[512,2048]{1,0:T(8,128)(2,1)} %xa_ref.1) | copy-start | bytes 6291460
  10.7 14.1 %copy-start.4 = (bf16[512,2048]{1,0:T(8,128)(2,1)S(1)}, bf16[512,2048]{1,0:T(8,128)(2,1)}, u32[]{:S(2)}) copy-start(bf16[512,2048]{1,0:T(8,128)(2,1)} %xb_ref.1) | copy-start | bytes 6291460
  10.7 14.2 %slice-start.1 = ((s8[8388608]{0:T(1024)(128)(4,1)}), s8[4194304]{0:T(1024)(128)(4,1)S(1)}, s32[]{:S(2)}) async-start(s8[8388608]{0:T(1024)(128)(4,1)} %bitcast.114), calls=%async_computation.5 | async-start | bytes 8388608
  10.7 25.0 %slice-start.2 = ((s8[8388608]{0:T(1024)(128)(4,1)}), s8[4194304]{0:T(1024)(128)(4,1)S(1)}, s32[]{:S(2)}) async-start(s8[8388608]{0:T(1024)(128)(4,1)} %bitcast.116), calls=%async_computation.6 | async-start | bytes 8388608
  24.9 10.9 %slice-start.3 = ((s8[8388608]{0:T(1024)(128)(4,1)}), s8[4194304]{0:T(1024)(128)(4,1)S(1)}, s32[]{:S(2)}) async-start(s8[8388608]{0:T(1024)(128)(4,1)} %bitcast.116), calls=%async_computation.7 | async-start | bytes 8388608
  35.7 11.1 %copy-start.7 = (s32[512,6]{0,1:T(8,128)S(1)}, s32[512,6]{0,1:T(8,128)}, u32[]{:S(2)}) copy-start(s32[512,6]{0,1:T(8,128)} %param.22) | copy-start | bytes 36868
  35.7 11.1 %copy-start.8 = (s32[512,6]{0,1:T(8,128)S(1)}, s32[512,6]{0,1:T(8,128)}, u32[]{:S(2)}) copy-start(s32[512,6]{0,1:T(8,128)} %param.26) | copy-start | bytes 36868
  35.8 11.4 %copy-start.9 = (s32[512,6]{0,1:T(8,128)S(1)}, s32[512,6]{0,1:T(8,128)}, u32[]{:S(2)}) copy-start(s32[512,6]{0,1:T(8,128)} %param.23) | copy-start | bytes 36868
  35.8 11.4 %copy-start.10 = (s32[512,6]{0,1:T(8,128)S(1)}, s32[512,6]{0,1:T(8,128)}, u32[]{:S(2)}) copy-start(s32[512,6]{0,1:T(8,128)} %param.27) | copy-start | bytes 36868
  35.8 16.7 %copy-start.11 = (bf16[2048]{0:T(1024)(128)(2,1)S(1)}, bf16[2048]{0:T(1024)(128)(2,1)}, u32[]{:S(2)}) copy-start(bf16[2048]{0:T(1024)(128)(2,1)} %param.34) | copy-start | bytes 12292
  51.8 0.6 copy-start.2
  53.1 98.7 %copy-start.5 = (bf16[512,6]{0,1:T(8,128)(2,1)S(1)}, bf16[512,6]{0,1:T(8,128)(2,1)}, u32[]{:S(2)}) copy-start(bf16[512,6]{0,1:T(8,128)(2,1)} %param.24) | copy-start | bytes 18436
  53.1 98.7 %copy-start.6 = (bf16[512,6]{0,1:T(8,128)(2,1)S(1)}, bf16[512,6]{0,1:T(8,128)(2,1)}, u32[]{:S(2)}) copy-start(bf16[512,6]{0,1:T(8,128)(2,1)} %param.28) | copy-start | bytes 18436
  152.0 105.7 %all-gather.7.cloned.1.call-start = ((), (), s32[]{:S(2)}) async-start(), calls=%async_computation.3 | async-start | bytes 18874368 | tf_op jit(solution)/shard_map/cond/branch_1_fun/all_gather | solution.py:933
  250.1 134.1 %all-to-all-start = ((bf16[8,352,2048]{2,1,0:T(8,128)(2,1)}), bf16[8,352,2048]{2,1,0:T(8,128)(2,1)}, u32[]{:S(2)}, u32[]{:S(2)}) async-start(bf16[8,352,2048]{2,1,0:T(8,128)(2,1)} %pack.7), calls=%async_computation | async-start | bytes 23068672 | tf_op jit(solution)/shard_map/cond/branch_1_fun/all_to_all | solution.py:935
  517.7 1.6 copy-start
  519.3 1.6 copy-start.1
Sparse Core Ops, SparseCore 0:
  154.4 83.6 all-gather.6
